TPU v7x, 16 devices: a whole 2x2x2 slice. The times are simulated.
16 devices in a mesh: dp: 4 (over z, y), ep: 4 (over x, core).
Axes of the slice: x: 2, y: 2, z: 2, core: 2. Of those that a mesh axis runs over, the one named last changes fastest.
Arguments:
- tokens: bfloat16 [4096, 1024], P(('dp', 'ep'))
- w_router: bfloat16 [1024, 32], replicated
- w_gate: bfloat16 [32, 1024, 512], P('ep')
- w_up: bfloat16 [32, 1024, 512], P('ep')
- w_down: bfloat16 [32, 512, 1024], P('ep')
- top_ids: int32 [4096, 8], P(('dp', 'ep'))
- r_proj: bfloat16 [4096, 1024], P(('dp', 'ep'))
Outputs:
- output 1: float32 [4096, 1024], P(('dp', 'ep'))
- output 2: float32 [4096, 1024], P(('dp', 'ep'))
- output 3: float32 [32, 1024, 512], P('ep')
- output 4: float32 [32, 1024, 512], P('ep')
- output 5: float32 [32, 512, 1024], P('ep')
- output 6: float32 [1024, 32], replicated
All inputs are finite; a program needn't handle non-finite values.
Results may differ from a plain program's by a relative error of at most 0.00174.
Values are sent between devices in bfloat16 or wider.
A program may use at most 1 GiB of HBM per device.

v0:
```python
import functools

import jax
import jax.numpy as jnp
from jax import lax
from jax.experimental import pallas as pl
from jax.experimental.pallas import tpu as pltpu
from jax.sharding import PartitionSpec as P


F32 = jnp.float32
BF16 = jnp.bfloat16
I32 = jnp.int32
GRP = 16
UNIT = 128
MOST = 4
STEP = 256
BLK = 256
PER = STEP // GRP
MESH = pl.DeviceIdType.MESH


def _dot(a, b, ca, cb):
    return lax.dot_general(a, b, (((ca,), (cb,)), ((), ())), preferred_element_type=F32)


def _flip(v, mask):
    for k in range(2):
        if (mask >> k) & 1:
            v = v + (1 << k) * (1 - 2 * ((v // (1 << k)) % 2))
    return v


def _peers(dp, ep, ep_size, n_dev):
    return {r: (_flip(dp, r // ep_size), _flip(ep, r % ep_size)) for r in range(1, n_dev)}


def _greet(peers):
    barrier = pltpu.get_barrier_semaphore()
    for peer in peers.values():
        pl.semaphore_signal(barrier, inc=1, device_id=peer, device_id_type=MESH)
    pl.semaphore_wait(barrier, len(peers))


def first_kernel(x_ref, wr_ref, ids_ref, xr_ref, own_ref, out_ref, b1, b2, b4, b8, b3, b5, b9, ssem, rsem, bsend, brecv, fsend, frecv, *, n_dev, ep_size):
    dp, ep = lax.axis_index('dp'), lax.axis_index('ep')
    peers = _peers(dp, ep, ep_size, n_dev)
    local = out_ref.shape[1]
    _greet(peers)

    def copy(src, dst, s, r, k, mask):
        return pltpu.make_async_remote_copy(src_ref=src, dst_ref=dst, send_sem=s.at[k], recv_sem=r.at[k], device_id=peers[mask], device_id_type=MESH)

    half = xr_ref.shape[0] // 2
    part = [pl.ds(0, half), pl.ds(half, half)]
    direct = []
    for h in range(2):
        for k, (dst, mask) in enumerate(((b2, 2), (b4, 4), (b8, 8), (b1, 1))):
            direct.append(copy(xr_ref.at[part[h], :], dst.at[part[h], :], bsend, brecv, 4 * h + k, mask))
            direct[-1].start()
    z = _dot(wr_ref[...], x_ref[...], 0, 1)
    eid = lax.broadcasted_iota(I32, z.shape, 0)
    sel = eid == ids_ref[0:1, :]
    for j in range(1, ids_ref.shape[0]):
        sel = jnp.logical_or(sel, eid == ids_ref[j : j + 1, :])
    peak = jnp.max(jnp.where(sel, z, -3.0e38), axis=0, keepdims=True)
    ex = jnp.where(sel, jnp.exp(jnp.where(sel, z - peak, 0.0)), 0.0)
    gates = ex / jnp.sum(ex, axis=0, keepdims=True)
    marked = jnp.where(sel, gates, -1.0)
    for k in range(ep_size):
        own_ref[k] = marked[k * local : (k + 1) * local, :]
    out_ref[0] = own_ref[ep]
    direct[3].wait_recv()
    small = [copy(own_ref.at[peer[1]], out_ref.at[r], ssem, rsem, r, r) for r, peer in peers.items()]
    for c in small:
        c.start()
    passed = []
    for h in range(2):
        for k, (src, dst) in enumerate(((b2, b3), (b4, b5), (b8, b9))):
            direct[4 * h + k].wait_recv()
            passed.append(copy(src.at[part[h], :], dst.at[part[h], :], fsend, frecv, 3 * h + k, 1))
            passed[-1].start()
    direct[7].wait_recv()
    for c in direct:
        c.wait_send()
    for c in passed + small:
        c.wait()


def first_stage(tokens, w_router, ids_t, xr, n_dev, ep_size):
    local = w_router.shape[1] // ep_size
    n_tok = tokens.shape[0]
    vmem = pl.BlockSpec(memory_space=pltpu.VMEM)
    hbm = pl.BlockSpec(memory_space=pl.ANY)
    dma = pltpu.SemaphoreType.DMA
    return pl.pallas_call(
        functools.partial(first_kernel, n_dev=n_dev, ep_size=ep_size),
        out_shape=[jax.ShapeDtypeStruct((ep_size, local, n_tok), F32), jax.ShapeDtypeStruct((n_dev, local, n_tok), F32)] + [jax.ShapeDtypeStruct(xr.shape, BF16)] * 7,
        in_specs=[vmem] * 3 + [hbm],
        out_specs=[vmem] * 2 + [hbm] * 7,
        scratch_shapes=[dma((n_dev,)), dma((n_dev,)), dma((8,)), dma((8,)), dma((6,)), dma((6,))],
        compiler_params=pltpu.CompilerParams(collective_id=0, has_side_effects=True),
        cost_estimate=pl.CostEstimate(flops=20_000_000_000, bytes_accessed=20_000_000, transcendentals=0),
        name='first_stage',
    )(tokens, w_router, ids_t, xr)


def last_kernel(b6, b10, b12, b7, b11, b13, b14, b15, ssem, rsem, *, n_dev, ep_size):
    dp, ep = lax.axis_index('dp'), lax.axis_index('ep')
    every = _peers(dp, ep, ep_size, n_dev)
    peers = {m: every[m] for m in (1, 2, 4, 8)}
    _greet(peers)

    def copy(src, dst, k, mask):
        return pltpu.make_async_remote_copy(src_ref=src, dst_ref=dst, send_sem=ssem.at[k], recv_sem=rsem.at[k], device_id=peers[mask], device_id_type=MESH)

    n_row = b6.shape[0]
    c0 = n_row // 3 // GRP * GRP + GRP
    c1 = (c0 + n_row) // 2 // GRP * GRP
    far = []
    for k, (src, mask, lo, hi) in enumerate(((b12, 2, 0, c0), (b10, 4, c0, c1), (b6, 8, c1, n_row))):
        far.append(copy(src.at[pl.ds(lo, hi - lo), :], b14.at[pl.ds(lo, hi - lo), :], k, mask))
        far[-1].start()
    near = [copy(src, dst, 3 + k, 1) for k, (src, dst) in enumerate(((b6, b7), (b10, b11), (b12, b13)))]
    for c in near:
        c.start()
    for c in far:
        c.wait_recv()
    end = copy(b14, b15, 6, 1)
    end.start()
    for c in far:
        c.wait_send()
    for c in near:
        c.wait()
    end.wait()


def last_stage(b6, b10, b12, n_dev, ep_size):
    hbm = pl.BlockSpec(memory_space=pl.ANY)
    return pl.pallas_call(
        functools.partial(last_kernel, n_dev=n_dev, ep_size=ep_size),
        out_shape=[jax.ShapeDtypeStruct(b6.shape, BF16)] * 5,
        in_specs=[hbm] * 3,
        out_specs=[hbm] * 5,
        scratch_shapes=[pltpu.SemaphoreType.DMA((7,)), pltpu.SemaphoreType.DMA((7,))],
        compiler_params=pltpu.CompilerParams(collective_id=2, has_side_effects=True),
        cost_estimate=pl.CostEstimate(flops=10_000_000_000, bytes_accessed=10_000_000, transcendentals=0),
        name='last_stage',
    )(b6, b10, b12)


def router_kernel(dg_ref, g_ref, x_ref, dz_ref, gr_ref, all_ref, part_ref, take_ref, sem_a, sem_b, sem_c, sem_d, sem_e, sem_f, *, n_dev, ep_size):
    dp, ep = lax.axis_index('dp'), lax.axis_index('ep')
    me = dp * ep_size + ep
    peers = _peers(dp, ep, ep_size, n_dev)
    all_ref[ep] = dg_ref[0]
    _greet(peers)
    copies = []
    for r in range(1, ep_size):
        copies.append(pltpu.make_async_remote_copy(src_ref=dg_ref.at[r], dst_ref=all_ref.at[ep], send_sem=sem_a.at[r], recv_sem=sem_b.at[r], device_id=peers[r], device_id_type=MESH))
        copies[-1].start()
    for c in copies:
        c.wait()
    g = jnp.maximum(jnp.concatenate([g_ref[k] for k in range(ep_size)], axis=0), 0.0)
    dg = jnp.concatenate([all_ref[k] for k in range(ep_size)], axis=0)
    dz = (g * (dg - jnp.sum(g * dg, axis=0, keepdims=True))).astype(BF16)
    dz_ref[...] = dz
    part = _dot(dz, x_ref[...], 1, 0)
    rows = part.shape[0] // n_dev
    for k in range(n_dev):
        part_ref[k] = part[k * rows : (k + 1) * rows, :]
    take_ref[me] = part_ref[me]
    copies = []
    for r, peer in peers.items():
        pid = peer[0] * ep_size + peer[1]
        copies.append(pltpu.make_async_remote_copy(src_ref=part_ref.at[pid], dst_ref=take_ref.at[me], send_sem=sem_c.at[r], recv_sem=sem_d.at[r], device_id=peer, device_id_type=MESH))
        copies[-1].start()
    for c in copies:
        c.wait()
    total = take_ref[0]
    for k in range(1, n_dev):
        total = total + take_ref[k]
    gr_ref[me] = total
    copies = []
    for r, peer in peers.items():
        copies.append(pltpu.make_async_remote_copy(src_ref=gr_ref.at[me], dst_ref=gr_ref.at[me], send_sem=sem_e.at[r], recv_sem=sem_f.at[r], device_id=peer, device_id_type=MESH))
        copies[-1].start()
    for c in copies:
        c.wait()


def router_backward(dg, gates, tokens, n_dev, ep_size):
    n_exp = gates.shape[0] * gates.shape[1]
    n_tok, hidden = tokens.shape
    vmem = pl.BlockSpec(memory_space=pltpu.VMEM)
    rows = n_exp // n_dev
    dma = pltpu.SemaphoreType.DMA((n_dev,))
    return pl.pallas_call(
        functools.partial(router_kernel, n_dev=n_dev, ep_size=ep_size),
        out_shape=[jax.ShapeDtypeStruct((n_exp, n_tok), BF16), jax.ShapeDtypeStruct((n_dev, rows, hidden), F32)],
        in_specs=[vmem] * 3,
        out_specs=[vmem] * 2,
        scratch_shapes=[
            pltpu.VMEM((ep_size, n_exp // ep_size, n_tok), F32),
            pltpu.VMEM((n_dev, rows, hidden), F32),
            pltpu.VMEM((n_dev, rows, hidden), F32),
            *([dma] * 6),
        ],
        compiler_params=pltpu.CompilerParams(collective_id=1, has_side_effects=True),
        cost_estimate=pl.CostEstimate(flops=2_000_000_000, bytes_accessed=2_000_000, transcendentals=0),
        name='router_backward',
    )(dg, gates, tokens)


def _slots(g_ref, start_ref, slot_ref):
    tri = (lax.broadcasted_iota(I32, (BLK, BLK), 0) < lax.broadcasted_iota(I32, (BLK, BLK), 1)).astype(F32).astype(BF16)
    sel = g_ref[...] >= 0.0
    pos = _dot(jnp.where(sel, 1.0, 0.0).astype(BF16), tri, 1, 0).astype(I32)
    slot_ref[...] = jnp.where(sel, pos + start_ref[...], -1)


def _onehot(code_ref, i, k, slot_ref, g_ref, hot_ref, gate_ref, n_exp):
    for q in range(PER):
        code = code_ref[i, k * PER + q]
        e = lax.rem(code, GRP)
        ids = lax.broadcasted_iota(I32, (GRP, BLK), 0) + (k * STEP + q * GRP)
        at = pl.ds(i * n_exp + e, 1)
        eq = slot_ref[at, :] == ids
        rows = slice(q * GRP, (q + 1) * GRP)
        hot_ref[rows, :] = jnp.where(eq, 1.0, 0.0).astype(BF16)
        gate_ref[rows, :] = jnp.where(eq, g_ref[at, :], 0.0)


def sort_kernel(meta_ref, code_ref, zero_ref, g_ref, start_ref, *rest, n_exp, n_blk, skip):
    srcs = rest[:n_blk]
    out_ref, slot_ref, x_ref, buf_ref, zbuf_ref, hot_ref, gate_ref, xsem, sem_ref, zsem = rest[n_blk:]
    hidden = x_ref.shape[2] // 2

    def zeros(q):
        return pltpu.make_async_copy(zbuf_ref, out_ref.at[pl.ds(pl.multiple_of(q * GRP, GRP), GRP), :], zsem.at[0])

    for k in range(n_blk):
        pltpu.make_async_copy(srcs[k], x_ref.at[k], xsem.at[k]).start()
    zbuf_ref[...] = jnp.zeros_like(zbuf_ref)
    for e in range(n_exp):
        lax.fori_loop(0, zero_ref[1, e], lambda q, c: (zeros(zero_ref[0, e] + q).start(), c)[1], 0)
    _slots(g_ref, start_ref, slot_ref)

    def drain(s, cnt):
        @pl.when(cnt == PER)
        def _():
            pltpu.make_async_copy(buf_ref.at[0], out_ref.at[pl.ds(0, STEP), :], sem_ref.at[s]).wait()

        @pl.when(cnt < PER)
        def _():
            def one(_, c):
                pltpu.make_async_copy(buf_ref.at[0, pl.ds(0, GRP), :], out_ref.at[pl.ds(0, GRP), :], sem_ref.at[s]).wait()
                return c

            lax.fori_loop(0, cnt, one, 0)

    def block(i, c):
        n_grp = meta_ref[skip + i]
        pltpu.make_async_copy(srcs[0], x_ref.at[i], xsem.at[i]).wait()

        def step(k, c):
            s, old, newer = c
            _onehot(code_ref, skip + i, k, slot_ref, g_ref, hot_ref, gate_ref, n_exp)
            gcol = jnp.sum(gate_ref[...], axis=1, keepdims=True)
            hot = hot_ref[...]
            drain(s, old)
            buf_ref[s, :, :hidden] = _dot(hot, x_ref[i, :, :hidden], 1, 0).astype(BF16)
            buf_ref[s, :, hidden:] = (gcol * _dot(hot, x_ref[i, :, hidden:], 1, 0)).astype(BF16)
            cnt = jnp.minimum(n_grp - k * PER, PER)

            def send(q, c):
                code = code_ref[skip + i, k * PER + q]
                dst = pl.multiple_of(code - lax.rem(code, GRP), GRP)
                pltpu.make_async_copy(buf_ref.at[s, pl.ds(pl.multiple_of(q * GRP, GRP), GRP), :], out_ref.at[pl.ds(dst, GRP), :], sem_ref.at[s]).start()
                return c

            @pl.when(cnt == PER)
            def _():
                for q in range(PER):
                    send(q, 0)

            @pl.when(cnt < PER)
            def _():
                lax.fori_loop(0, cnt, send, 0)

            return 1 - s, newer, cnt

        return lax.fori_loop(0, (n_grp + PER - 1) // PER, step, c)

    s, old, newer = lax.fori_loop(0, n_blk, block, (jnp.int32(0), jnp.int32(0), jnp.int32(0)))
    drain(s, old)
    drain(1 - s, newer)
    for e in range(n_exp):
        lax.fori_loop(0, zero_ref[1, e], lambda q, c: (zeros(0).wait(), c)[1], 0)


def sort_rows(meta, code, zero, gates, start, blocks, skip, rows, n_exp):
    n_blk = len(blocks)
    width = blocks[0].shape[1]
    smem = pl.BlockSpec(memory_space=pltpu.SMEM)
    vmem = pl.BlockSpec(memory_space=pltpu.VMEM)
    hbm = pl.BlockSpec(memory_space=pl.ANY)
    return pl.pallas_call(
        functools.partial(sort_kernel, n_exp=n_exp, n_blk=n_blk, skip=skip),
        out_shape=jax.ShapeDtypeStruct((rows, width), BF16),
        in_specs=[smem] * 3 + [vmem] * 2 + [hbm] * n_blk,
        out_specs=hbm,
        scratch_shapes=[
            pltpu.VMEM(gates.shape, I32),
            pltpu.VMEM((n_blk, BLK, width), BF16),
            pltpu.VMEM((2, STEP, width), BF16),
            pltpu.VMEM((GRP, width), BF16),
            pltpu.VMEM((STEP, BLK), BF16),
            pltpu.VMEM((STEP, BLK), F32),
            pltpu.SemaphoreType.DMA((n_blk,)),
            pltpu.SemaphoreType.DMA((2,)),
            pltpu.SemaphoreType.DMA((1,)),
        ],
        cost_estimate=pl.CostEstimate(flops=1_500_000_000 * n_blk, bytes_accessed=3_000_000 * n_blk, transcendentals=0),
    )(meta, code, zero, gates, start, *blocks)


def _units(first, n, src_ref, buf_ref, sem, slot, op):
    for j in range(MOST):

        @pl.when(j < n)
        def _():
            row = pl.multiple_of((first + j) * UNIT, UNIT)
            op(pltpu.make_async_copy(src_ref.at[pl.ds(row, UNIT), :], buf_ref.at[slot, pl.ds(j * UNIT, UNIT), :], sem.at[slot]))


def _start(c):
    c.start()


def _wait(c):
    c.wait()


def _piece(n, k):
    cuts = (n + MOST - 1) // MOST
    low = n // cuts
    extra = n - low * cuts
    return k * low + jnp.minimum(k, extra), low + jnp.where(k < extra, 1, 0), cuts


def _next(t_ref, e, k, cuts, n_exp):
    here = _piece(t_ref[1, e], jnp.minimum(k + 1, cuts - 1))[1]
    there = jnp.where(e + 1 < n_exp, _piece(t_ref[1, jnp.minimum(e + 1, n_exp - 1)], 0)[1], 0)
    return jnp.where(k + 1 < cuts, here, there)


def _hidden(u, d, w1_ref, w3_ref, w2_ref, j, w):
    h1 = _dot(u, w1_ref[0, :, j : j + w], 1, 0)
    h3 = _dot(u, w3_ref[0, :, j : j + w], 1, 0)
    da = _dot(d, w2_ref[0, j : j + w, :], 1, 1)
    sig = jax.nn.sigmoid(h1)
    silu = h1 * sig
    act = (silu * h3).astype(BF16)
    dh1 = (da * h3 * sig * (1.0 + h1 * (1.0 - sig))).astype(BF16)
    dh3 = (da * silu).astype(BF16)
    return act, dh1, dh3


def own_kernel(t_ref, ud_ref, w1_ref, w3_ref, w2_ref, o_ref, sv_ref, in_ref, ob_ref, sb_ref, cnt_ref, isem, osem, ssem, *, n_exp, hidden, inner):
    e = pl.program_id(0)

    def put(g, n, s, op):
        for j in range(MOST):

            @pl.when(j < n)
            def _():
                rows = pl.ds(pl.multiple_of((g + j) * UNIT, UNIT), UNIT)
                op(pltpu.make_async_copy(ob_ref.at[s, pl.ds(j * UNIT, UNIT), :], o_ref.at[rows, :], osem.at[s]))
                op(pltpu.make_async_copy(sb_ref.at[s, pl.ds(j * UNIT, UNIT), :], sv_ref.at[rows, :], ssem.at[s]))

    @pl.when(e == 0)
    def _():
        cnt_ref[0] = 0
        cnt_ref[1] = 0
        cnt_ref[2] = 0
        _units(0, _piece(t_ref[1, 0], 0)[1], ud_ref, in_ref, isem, 0, _start)

    def piece(k, c):
        off, n, cuts = _piece(t_ref[1, e], k)
        g = t_ref[0, e] + off
        s = lax.rem(cnt_ref[2], 2)
        cnt_ref[2] = cnt_ref[2] + 1
        _units(g, n, ud_ref, in_ref, isem, s, _wait)
        _units(g + n, _next(t_ref, e, k, cuts, n_exp), ud_ref, in_ref, isem, 1 - s, _start)
        put(0, cnt_ref[s], s, _wait)
        cnt_ref[s] = n
        for size in range(1, MOST + 1):

            @pl.when(n == size)
            def _():
                r = size * UNIT
                for j in range(0, inner, 256):
                    act, dh1, dh3 = _hidden(in_ref[s, :r, :hidden], in_ref[s, :r, hidden:], w1_ref, w3_ref, w2_ref, j, 256)
                    sb_ref[s, :r, j : j + 256] = act
                    sb_ref[s, :r, inner + j : inner + j + 256] = dh1
                    sb_ref[s, :r, 2 * inner + j : 2 * inner + j + 256] = dh3
                ob_ref[s, :r, :hidden] = _dot(sb_ref[s, :r, :inner], w2_ref[0], 1, 0).astype(BF16)
                ob_ref[s, :r, hidden:] = (_dot(sb_ref[s, :r, inner : 2 * inner], w1_ref[0], 1, 1) + _dot(sb_ref[s, :r, 2 * inner :], w3_ref[0], 1, 1)).astype(BF16)

        put(g, n, s, _start)
        return c

    lax.fori_loop(0, (t_ref[1, e] + MOST - 1) // MOST, piece, 0)

    @pl.when(e == n_exp - 1)
    def _():
        for s in range(2):
            put(0, cnt_ref[s], s, _wait)


def own_rows(table, ud, w1, w3, w2):
    n_exp, hidden, inner = w1.shape
    n_row, width = ud.shape
    wspec = lambda a, b: pl.BlockSpec((1, a, b), lambda e, t: (e, 0, 0))
    hbm = pl.BlockSpec(memory_space=pl.ANY)
    spec = pltpu.PrefetchScalarGridSpec(
        num_scalar_prefetch=1,
        grid=(n_exp,),
        in_specs=[hbm, wspec(hidden, inner), wspec(hidden, inner), wspec(inner, hidden)],
        out_specs=[hbm, hbm],
        scratch_shapes=[
            pltpu.VMEM((2, MOST * UNIT, width), BF16),
            pltpu.VMEM((2, MOST * UNIT, width), BF16),
            pltpu.VMEM((2, MOST * UNIT, 3 * inner), BF16),
            pltpu.SMEM((3,), I32),
            pltpu.SemaphoreType.DMA((2,)),
            pltpu.SemaphoreType.DMA((2,)),
            pltpu.SemaphoreType.DMA((2,)),
        ],
    )
    return pl.pallas_call(
        functools.partial(own_kernel, n_exp=n_exp, hidden=hidden, inner=inner),
        out_shape=[jax.ShapeDtypeStruct((n_row, width), BF16), jax.ShapeDtypeStruct((n_row, 3 * inner), BF16)],
        grid_spec=spec,
        name='own_rows',
        cost_estimate=pl.CostEstimate(flops=30_000_000_000, bytes_accessed=60_000_000, transcendentals=2_000_000),
    )(table, ud, w1, w3, w2)


def grads_kernel(ta_ref, tb_ref, uo_ref, sv_ref, ud_ref, w1_ref, w3_ref, w2_ref, g1_ref, g3_ref, g2_ref, oin_ref, sin_ref, in_ref, act_ref, dh_ref, cnt_ref, osem, ssem, isem, *, n_exp, hidden, inner):
    e = pl.program_id(0)

    @pl.when(e == 0)
    def _():
        cnt_ref[0] = 0
        cnt_ref[1] = 0
        n = _piece(ta_ref[1, 0], 0)[1]
        _units(0, n, uo_ref, oin_ref, osem, 0, _start)
        _units(0, n, sv_ref, sin_ref, ssem, 0, _start)
        _units(0, _piece(tb_ref[1, 0], 0)[1], ud_ref, in_ref, isem, 0, _start)

    mc = 256

    def outer(x_ref, s, r, act, dh1, dh3, fresh):
        def put(ref, m, v):
            ref[0, m : m + mc, :] = v if fresh else ref[0, m : m + mc, :] + v

        for m in range(0, hidden, mc):
            u = x_ref[s, :r, m : m + mc]
            put(g1_ref, m, _dot(u, dh1, 0, 0))
            put(g3_ref, m, _dot(u, dh3, 0, 0))
        d = x_ref[s, :r, hidden:]
        for m in range(0, inner, mc):
            put(g2_ref, m, _dot(act[:, m : m + mc], d, 0, 0))

    def own_piece(k, c):
        off, n, cuts = _piece(ta_ref[1, e], k)
        g = ta_ref[0, e] + off
        s = lax.rem(cnt_ref[0], 2)
        cnt_ref[0] = cnt_ref[0] + 1
        _units(g, n, uo_ref, oin_ref, osem, s, _wait)
        _units(g, n, sv_ref, sin_ref, ssem, s, _wait)
        m = _next(ta_ref, e, k, cuts, n_exp)
        _units(g + n, m, uo_ref, oin_ref, osem, 1 - s, _start)
        _units(g + n, m, sv_ref, sin_ref, ssem, 1 - s, _start)
        for size, fresh in [(v, True) for v in range(1, MOST + 1)] + [(v, False) for v in range(2, MOST + 1)]:

            @pl.when(jnp.logical_and(n == size, (k == 0) == fresh))
            def _():
                r = size * UNIT
                outer(oin_ref, s, r, sin_ref[s, :r, :inner], sin_ref[s, :r, inner : 2 * inner], sin_ref[s, :r, 2 * inner :], fresh)

        return c

    lax.fori_loop(0, (ta_ref[1, e] + MOST - 1) // MOST, own_piece, 0)

    def piece(k, c):
        off, n, cuts = _piece(tb_ref[1, e], k)
        g = tb_ref[0, e] + off
        s = lax.rem(cnt_ref[1], 2)
        cnt_ref[1] = cnt_ref[1] + 1
        _units(g, n, ud_ref, in_ref, isem, s, _wait)
        _units(g + n, _next(tb_ref, e, k, cuts, n_exp), ud_ref, in_ref, isem, 1 - s, _start)
        for size in range(1, MOST + 1):

            @pl.when(n == size)
            def _():
                r = size * UNIT
                for j in range(0, inner, mc):
                    act, dh1, dh3 = _hidden(in_ref[s, :r, :hidden], in_ref[s, :r, hidden:], w1_ref, w3_ref, w2_ref, j, mc)
                    act_ref[:r, j : j + mc] = act
                    dh_ref[:r, j : j + mc] = dh1
                    dh_ref[:r, inner + j : inner + j + mc] = dh3
                outer(in_ref, s, r, act_ref[:r, :], dh_ref[:r, :inner], dh_ref[:r, inner:], False)

        return c

    lax.fori_loop(0, (tb_ref[1, e] + MOST - 1) // MOST, piece, 0)


def weight_grads(ta, tb, uo, sv, ud, w1, w3, w2):
    n_exp, hidden, inner = w1.shape
    width = ud.shape[1]
    wspec = lambda a, b: pl.BlockSpec((1, a, b), lambda e, t, s: (e, 0, 0))
    hbm = pl.BlockSpec(memory_space=pl.ANY)
    most = MOST * UNIT
    spec = pltpu.PrefetchScalarGridSpec(
        num_scalar_prefetch=2,
        grid=(n_exp,),
        in_specs=[hbm, hbm, hbm, wspec(hidden, inner), wspec(hidden, inner), wspec(inner, hidden)],
        out_specs=[wspec(hidden, inner), wspec(hidden, inner), wspec(inner, hidden)],
        scratch_shapes=[
            pltpu.VMEM((2, most, width), BF16),
            pltpu.VMEM((2, most, 3 * inner), BF16),
            pltpu.VMEM((2, most, width), BF16),
            pltpu.VMEM((most, inner), BF16),
            pltpu.VMEM((most, 2 * inner), BF16),
            pltpu.SMEM((2,), I32),
            pltpu.SemaphoreType.DMA((2,)),
            pltpu.SemaphoreType.DMA((2,)),
            pltpu.SemaphoreType.DMA((2,)),
        ],
    )
    return pl.pallas_call(
        functools.partial(grads_kernel, n_exp=n_exp, hidden=hidden, inner=inner),
        out_shape=[jax.ShapeDtypeStruct(w.shape, F32) for w in (w1, w3, w2)],
        grid_spec=spec,
        name='weight_grads',
        cost_estimate=pl.CostEstimate(flops=90_000_000_000, bytes_accessed=150_000_000, transcendentals=4_000_000),
    )(ta, tb, uo, sv, ud, w1, w3, w2)


def combine_kernel(meta_ref, code_ref, g_ref, start_ref, r_ref_a, r_ref_b, o_ref, *rest, n_exp, hidden, which, more):
    if more:
        add_ref, keep_ref, go_ref, dg_ref, p_ref, slot_ref, buf_ref, hot_ref, gate_ref, sem_ref = rest
    else:
        p_ref, dg_ref, slot_ref, buf_ref, hot_ref, gate_ref, sem_ref = rest
    i = pl.program_id(0)

    def rel(k):
        return which[0] + k * (which[1] - which[0])

    def pull(k, s):
        def one(q, c):
            code = code_ref[rel(k), q]
            src = pl.multiple_of(code - lax.rem(code, GRP), GRP)
            pltpu.make_async_copy(o_ref.at[pl.ds(src, GRP), :], buf_ref.at[s, pl.ds(pl.multiple_of(q * GRP, GRP), GRP), :], sem_ref.at[s]).start()
            return c

        lax.fori_loop(0, meta_ref[rel(k)], one, 0)

    @pl.when(i == 0)
    def _():
        pull(0, 0)
        pull(1, 1)
        _slots(g_ref, start_ref, slot_ref)

    n_grp = meta_ref[rel(i)]
    n_step = (n_grp + PER - 1) // PER

    def blank(q, c):
        buf_ref[i, pl.ds(pl.multiple_of(q * GRP, GRP), GRP), :] = jnp.zeros((GRP, buf_ref.shape[2]), BF16)
        return c

    lax.fori_loop(n_grp, n_step * PER, blank, 0)
    if more:
        p_ref[...] = add_ref[...]
    else:
        p_ref[...] = jnp.zeros_like(p_ref)
    dg_ref[...] = jnp.zeros_like(dg_ref)

    def whole(q, c):
        pltpu.make_async_copy(o_ref.at[pl.ds(0, STEP), :], buf_ref.at[0, pl.ds(0, STEP), :], sem_ref.at[i]).wait()
        return c

    def single(q, c):
        pltpu.make_async_copy(o_ref.at[pl.ds(0, GRP), :], buf_ref.at[0, pl.ds(0, GRP), :], sem_ref.at[i]).wait()
        return c

    lax.fori_loop(0, n_grp // PER, whole, 0)
    lax.fori_loop(0, lax.rem(n_grp, PER), single, 0)

    def step(k, c):
        rows = pl.ds(pl.multiple_of(k * STEP, STEP), STEP)
        o = buf_ref[i, rows, :hidden]
        rg = buf_ref[i, rows, hidden:]
        prod = _dot(o, jnp.where(i == 0, r_ref_a[...], r_ref_b[...]), 1, 1)
        _onehot(code_ref, rel(i), k, slot_ref, g_ref, hot_ref, gate_ref, n_exp)
        hot = hot_ref[...]
        prod = jnp.where(hot.astype(F32) > 0.5, prod, 0.0)
        for q in range(PER):
            e = lax.rem(code_ref[rel(i), k * PER + q], GRP)
            dg_ref[0, pl.ds(e, 1), :] += jnp.sum(prod[q * GRP : (q + 1) * GRP, :], axis=0, keepdims=True)
        gsel = gate_ref[...]
        g_hi = gsel.astype(BF16)
        rest = gsel - g_hi.astype(F32)
        g_mid = rest.astype(BF16)
        g_lo = (rest - g_mid.astype(F32)).astype(BF16)
        p_ref[:, :hidden] += _dot(g_hi, o, 0, 0) + (_dot(g_mid, o, 0, 0) + _dot(g_lo, o, 0, 0))
        p_ref[:, hidden:] += _dot(hot, rg, 0, 0)
        return c

    lax.fori_loop(0, n_step, step, 0)
    if more:

        @pl.when(i == 0)
        def _():
            keep_ref[...] = p_ref[...]

        @pl.when(i == 1)
        def _():
            go_ref[...] = p_ref[...]


def combine(meta, code, gates, start, blocks, o_rows, which, n_exp, add=None):
    width = o_rows.shape[1]
    hidden = width // 2
    half = pl.BlockSpec((BLK, hidden), lambda i, m, s: (0, 1))
    block = pl.BlockSpec((BLK, width), lambda i, m, s: (i, 0))
    more = [] if add is None else [add]
    whole = pl.BlockSpec(gates.shape, lambda i, m, s: (0, 0))
    fixed = pl.BlockSpec((BLK, width), lambda i, m, s: (0, 0))
    spec = pltpu.PrefetchScalarGridSpec(
        num_scalar_prefetch=2,
        grid=(2,),
        in_specs=[
            whole,
            whole,
            half,
            half,
            pl.BlockSpec(memory_space=pl.ANY),
            *([block] * len(more)),
        ],
        out_specs=([fixed] * 2 if more else [block]) + [pl.BlockSpec((1, n_exp, BLK), lambda i, m, s: (i, 0, 0))],
        scratch_shapes=[
            *([pltpu.VMEM((BLK, width), F32)] * len(more)),
            pltpu.VMEM(gates.shape, I32),
            pltpu.VMEM((2, BLK * n_exp, width), BF16),
            pltpu.VMEM((STEP, BLK), BF16),
            pltpu.VMEM((STEP, BLK), F32),
            pltpu.SemaphoreType.DMA((2,)),
        ],
    )
    return pl.pallas_call(
        functools.partial(combine_kernel, n_exp=n_exp, hidden=hidden, which=which, more=bool(more)),
        out_shape=([jax.ShapeDtypeStruct((BLK, width), F32)] * 2 if more else [jax.ShapeDtypeStruct((2 * BLK, width), F32)]) + [jax.ShapeDtypeStruct((2, n_exp, BLK), F32)],
        grid_spec=spec,
        name='combine',
        cost_estimate=pl.CostEstimate(flops=8_000_000_000, bytes_accessed=20_000_000, transcendentals=0),
    )(meta, code, gates, start, blocks[which[0]], blocks[which[1]], o_rows, *more)


def routing_tables(cnt, n_own):
    n_blk, n_exp = cnt.shape
    pad = (cnt + GRP - 1) // GRP * GRP
    before_e = (jnp.arange(n_exp)[:, None] < jnp.arange(n_exp)[None, :]).astype(I32)
    blk = jnp.arange(n_blk)
    same = (blk[:, None] < n_own) == (blk[None, :] < n_own)
    before_b = ((blk[:, None] < blk[None, :]) & same).astype(I32)
    blk_start = jnp.sum(pad[:, :, None] * before_e[None], axis=1)
    blk_end = blk_start + pad
    in_exp = jnp.sum(pad[:, None, :] * before_b[:, :, None], axis=0)

    def part(p):
        total = jnp.sum(p, axis=0)
        units = jnp.maximum((total + UNIT - 1) // UNIT, 1)
        first = jnp.sum(units[:, None] * before_e, axis=0)
        zero = jnp.stack([(first * UNIT + total) // GRP, (units * UNIT - total) // GRP])
        return jnp.stack([first, units]).astype(I32), zero.astype(I32), first * UNIT

    ta, za, base_a = part(pad[:n_own])
    tb, zb, base_b = part(pad[n_own:])
    base = jnp.where(blk[:, None] < n_own, base_a[None], base_b[None])
    q = jnp.arange(BLK * n_exp // GRP, dtype=I32) * GRP
    inside = (q[None, :, None] >= blk_start[:, None, :]) & (q[None, :, None] < blk_end[:, None, :])
    place = base + in_exp - blk_start + jnp.arange(n_exp, dtype=I32)[None]
    code = jnp.sum(jnp.where(inside, place[:, None, :] + q[None, :, None], 0), axis=2)
    start = jnp.broadcast_to(blk_start.reshape(n_blk * n_exp, 1), (n_blk * n_exp, BLK)).astype(I32)
    return (jnp.sum(pad, axis=1) // GRP).astype(I32), start, code.astype(I32), ta, za, tb, zb


def solution(mesh):
    ep_size = mesh.shape['ep']
    dp_size = mesh.shape['dp']
    n_dev = ep_size * dp_size
    all_axes = ('dp', 'ep')

    def swap(v, mask):
        return lax.ppermute(v, all_axes, [(d, d ^ mask) for d in range(n_dev)])

    def layer(tokens, w_router, w_gate, w_up, w_down, top_ids, r_proj):
        n_local, hidden = tokens.shape
        n_exp = w_router.shape[1]
        local_exp = w_gate.shape[0]
        xr = jnp.concatenate([tokens, r_proj], axis=1)
        blk = {0: xr}
        own_gates, gates, *got = first_stage(tokens, w_router, top_ids.T, xr, n_dev, ep_size)
        blk.update(zip((1, 2, 4, 8, 3, 5, 9), got))
        for dst, src, mask in ((6, 4, 2), (12, 8, 4), (10, 2, 8)):
            blk[dst] = swap(blk[src], mask)
        cnt = jnp.sum((gates >= 0).astype(I32), axis=2)
        gates = gates.reshape(n_dev * local_exp, n_local)
        meta, start, code, ta, za, tb, zb = routing_tables(cnt, ep_size)
        own_n = ep_size * n_local * local_exp + local_exp * UNIT
        oth_n = (n_dev - ep_size) * n_local * local_exp + local_exp * UNIT
        uo = sort_rows(meta, code, za, gates, start, [blk[k] for k in range(4)], 0, own_n, local_exp)
        o_rows, sv = own_rows(ta, uo, w_gate, w_up, w_down)
        p_send, dg_b = combine(meta, code, gates, start, blk, o_rows, (1, 3), local_exp)
        p_sib = swap(p_send, 1)
        late = [blk[6], blk[10], blk[12]]
        p_send, *late = lax.optimization_barrier((p_send, *late))
        blk[6], blk[10], blk[12] = late
        blk[7], blk[11], blk[13], blk[14], blk[15] = last_stage(*late, n_dev, ep_size)
        ud = sort_rows(meta, code, zb, gates, start, [blk[k] for k in range(4, 16)], 4, oth_n, local_exp)
        p_sib, ud = lax.optimization_barrier((p_sib, ud))
        p_keep, p_go, dg_a = combine(meta, code, gates, start, blk, o_rows, (0, 2), local_exp, p_sib)
        dg = jnp.stack([dg_a[0], dg_b[0], dg_a[1], dg_b[1]])
        dz_t, grad_router_t = router_backward(dg, own_gates, tokens, n_dev, ep_size)
        p_go, dz_t = lax.optimization_barrier((p_go, dz_t))
        p_far = swap(p_go, 2)
        g_gate, g_up, g_down = weight_grads(ta, tb, uo, sv, ud, w_gate, w_up, w_down)
        grad_router = grad_router_t.reshape(n_exp, hidden).T
        y = tokens.astype(F32) + (p_keep[:, :hidden] + p_far[:, :hidden])
        dx = r_proj.astype(F32) + _dot(dz_t, w_router, 0, 1) + (p_keep[:, hidden:] + p_far[:, hidden:])
        return y, dx, g_gate, g_up, g_down, grad_router

    tok_spec = P(all_axes, None)
    exp_spec = P('ep', None, None)
    return jax.shard_map(layer, mesh=mesh, in_specs=(tok_spec, P(), exp_spec, exp_spec, exp_spec, tok_spec, tok_spec), out_specs=(tok_spec, tok_spec, exp_spec, exp_spec, exp_spec, P()), check_vma=False)
```

profile of v0, /device:TPU:1, one launch (start us, length us, event | category | flops | bytes accessed | tf_op | source)
XLA Modules:
  0.0 326.4 jit_solution(6401639443882542298)
XLA Ops:
  0.7 1.7 copy.21.wr_ref
  2.3 1.1 constant_dynamic-update-slice_fusion.1
  3.4 1.1 constant_dynamic-update-slice_fusion.xr_ref.rest_0_.r_ref_a
  4.5 1.0 copy-done
  5.5 35.5 %first_stage.1 = (f32[4,8,256]{2,1,0:T(8,128)}, f32[16,8,256]{2,1,0:T(8,128)}, bf16[256,2048]{1,0:T(8,128)(2,1)}, bf16[256,2048]{1,0:T(8,128)(2,1)}, bf16[256,20...) custom-call(bf16[256,1024]{1,0:T(8,128)(2,1)} %x_ref.3, ...), custom_call_target="tpu_custom_call" | custom-call | flops 20000000000 | bytes 20000000 | tf_op jit(solution)/shard_map/first_stage/pallas_call | solution.py:96
  41.0 1.3 convert_reduce_fusion
  43.8 0.7 select_reduce_fusion.code_ref
  45.1 0.7 broadcast_in_dim.36.start_ref
  45.9 14.2 %shard_map.118.ud_ref.uo_ref = bf16[9216,2048]{1,0:T(8,128)(2,1)} custom-call(s32[16]{0:T(128)} %and_select_fusion.8.meta_ref, s32[16,128]{1,0:T(8,128)} %select_reduce_fusion.code_ref, s32[2,8]{1,0:T(2,128)} %get-tuple-element.87.zero_ref, f32[128,256]{1,0:T(8,128)} %bitcast.37, s32[128,256]{1,0:T(8,128)} %broadcast_in_dim.36.start_ref, ...), custom_call_target="tpu_custom_call" | custom-call | flops 6000000000 | bytes 12000000 | tf_op jit(solution)/shard_map/pallas_call | solution.py:308
  60.1 36.3 %own_rows.1 = (bf16[9216,2048]{1,0:T(8,128)(2,1)}, bf16[9216,1536]{1,0:T(8,128)(2,1)}) custom-call(s32[2,8]{1,0:T(2,128)} %get-tuple-element.86.t_ref.ta_ref, bf16[9216,2048]{1,0:T(8,128)(2,1)} %shard_map.118.ud_ref.uo_ref, bf16[8,1024,512]{2,1,0:T(8,128)(2,1)} %w1_ref.3, bf16[8,1024,512]{2,1,0:T(8,128)(2,1)} %w3_ref.3, bf16[8,512,1024]{2,1,0:T(8,128)(2,1)} %w2_ref.3), custom_call_target="tpu_custom_call" | custom-call | flops 30000001024 | bytes 60000000 | tf_op jit(solution)/shard_map/own_rows/pallas_call | solution.py:442
  96.4 14.0 %combine.2 = (f32[512,2048]{1,0:T(8,128)}, f32[2,8,256]{2,1,0:T(8,128)}) custom-call(s32[16]{0:T(128)} %and_select_fusion.8.meta_ref, s32[16,128]{1,0:T(8,128)} %select_reduce_fusion.code_ref, f32[128,256]{1,0:T(8,128)} %bitcast.38, s32[128,256]{1,0:T(8,128)} %broadcast_in_dim.36.start_ref, bf16[256,2048]{1,0:T(8,128)(2,1)} %get-tuple-element.41.rest_1_.r_ref_a, ...), custom_call_target="tpu_custom_call" | custom-call | flops 8000000000 | bytes 20000000 | tf_op jit(solution)/shard_map/combine/pallas_call | solution.py:665
  111.8 0.7 fusion.15
  112.6 22.4 %collective-permute-done.1.b6.rest_2_ = bf16[256,2048]{1,0:T(8,128)(2,1)S(1)} collective-permute-done((bf16[256,2048]{1,0:T(8,128)(2,1)S(1)}, bf16[256,2048]{1,0:T(8,128)(2,1)S(1)}, u32[]{:S(2)}, u32[]{:S(2)}) %collective-permute-start.1) | collective-permute-done | bytes 1048608 | tf_op jit(solution)/shard_map/ppermute | solution.py:710
  135.0 1.0 copy-done.8
  135.9 1.0 copy-done.7
  136.9 14.5 %last_stage.1 = (bf16[256,2048]{1,0:T(8,128)(2,1)}, bf16[256,2048]{1,0:T(8,128)(2,1)}, bf16[256,2048]{1,0:T(8,128)(2,1)}, bf16[256,2048]{1,0:T(8,128)(2,1)}, bf16[256,2048]{1,0:T(8,128)(2,1)}) custom-call(bf16[256,2048]{1,0:T(8,128)(2,1)} %copy-done.8, bf16[256,2048]{1,0:T(8,128)(2,1)} %copy-done.7, bf16[256,2048]{1,0:T(8,128)(2,1)} %collective-permute-done.3.b12.rest_8_), custom_call_target="tpu_custom_call" | custom-call | flops 10000000000 | bytes 10000000 | tf_op jit(solution)/shard_map/last_stage/pallas_call | solution.py:140
  151.4 33.2 %shard_map.119.ud_ref = bf16[25600,2048]{1,0:T(8,128)(2,1)} custom-call(s32[16]{0:T(128)} %and_select_fusion.8.meta_ref, s32[16,128]{1,0:T(8,128)} %select_reduce_fusion.code_ref, s32[2,8]{1,0:T(2,128)} %pad_add_fusion.2.zero_ref, f32[128,256]{1,0:T(8,128)} %bitcast.39, s32[128,256]{1,0:T(8,128)} %broadcast_in_dim.36.start_ref, ...), custom_call_target="tpu_custom_call" | custom-call | flops 17999998976 | bytes 36000000 | tf_op jit(solution)/shard_map/pallas_call | solution.py:308
  184.6 13.4 %combine.3 = (f32[256,2048]{1,0:T(8,128)}, f32[256,2048]{1,0:T(8,128)}, f32[2,8,256]{2,1,0:T(8,128)}) custom-call(s32[16]{0:T(128)} %and_select_fusion.8.meta_ref, s32[16,128]{1,0:T(8,128)} %select_reduce_fusion.code_ref, f32[128,256]{1,0:T(8,128)} %bitcast.40, s32[128,256]{1,0:T(8,128)} %broadcast_in_dim.36.start_ref, bf16[256,2048]{1,0:T(8,128)(2,1)} %copy-done, ...), custom_call_target="tpu_custom_call" | custom-call | flops 8000000000 | bytes 20000000 | tf_op jit(solution)/shard_map/combine/pallas_call | solution.py:665
  198.0 0.7 fusion.14
  199.4 17.3 %router_backward.1 = (bf16[32,256]{1,0:T(8,128)(2,1)}, f32[16,2,1024]{2,1,0:T(2,128)}) custom-call(f32[4,8,256]{2,1,0:T(8,128)} %pad_maximum_fusion.dg_ref, f32[4,8,256]{2,1,0:T(8,128)} %get-tuple-element.62.g_ref, bf16[256,1024]{1,0:T(8,128)(2,1)} %x_ref.3), custom_call_target="tpu_custom_call" | custom-call | flops 2000000000 | bytes 2000000 | tf_op jit(solution)/shard_map/router_backward/pallas_call | solution.py:198
  217.1 103.5 %weight_grads.1 = (f32[8,1024,512]{2,1,0:T(8,128)}, f32[8,1024,512]{2,1,0:T(8,128)}, f32[8,512,1024]{2,1,0:T(8,128)}) custom-call(s32[2,8]{1,0:T(2,128)} %get-tuple-element.86.t_ref.ta_ref, s32[2,8]{1,0:T(2,128)} %pad_add_fusion.3.tb_ref, bf16[9216,2048]{1,0:T(8,128)(2,1)} %shard_map.118.ud_ref.uo_ref, bf16[9216,1536]{1,0:T(8,128)(2,1)} %get-tuple-element.66.sv_ref, ...), custom_call_target="tpu_custom_call" | custom-call | flops 89999998976 | bytes 150000000 | tf_op jit(solution)/shard_map/weight_grads/pallas_call | solution.py:545
  320.7 0.7 reshape.559
  321.4 2.4 fusion.1
  323.9 2.5 fusion
  (57 shorter events, 4.5 us)
Async XLA Ops:
  4.5 1.0 copy-start
  96.4 14.1 %copy-start.1 = (bf16[256,2048]{1,0:T(8,128)(2,1)S(1)}, bf16[256,2048]{1,0:T(8,128)(2,1)}, u32[]{:S(2)}) copy-start(bf16[256,2048]{1,0:T(8,128)(2,1)} %get-tuple-element.40.rest_2_.r_ref_b) | copy-start | bytes 3145732
  96.4 14.2 %copy-start.5 = (bf16[256,2048]{1,0:T(8,128)(2,1)S(1)}, bf16[256,2048]{1,0:T(8,128)(2,1)}, u32[]{:S(2)}) copy-start(bf16[256,2048]{1,0:T(8,128)(2,1)} %get-tuple-element.45.rest_0_) | copy-start | bytes 3145732
  96.4 14.2 %copy-start.6 = (bf16[256,2048]{1,0:T(8,128)(2,1)S(1)}, bf16[256,2048]{1,0:T(8,128)(2,1)}, u32[]{:S(2)}) copy-start(bf16[256,2048]{1,0:T(8,128)(2,1)} %get-tuple-element.47.rest_4_) | copy-start | bytes 3145732
  110.4 74.2 %collective-permute-start = (f32[512,2048]{1,0:T(8,128)}, f32[512,2048]{1,0:T(8,128)}, u32[]{:S(2)}, u32[]{:S(2)}) collective-permute-start(f32[512,2048]{1,0:T(8,128)} %get-tuple-element.44), channel_id=1, source_target_pairs={{0,1},{1,0},{2,3},{3,2},{4,5},{5,4},{6,7},{7,6},{8,9},{9,8},{10,11... | collective-permute-start | bytes 12582920 | tf_op jit(solution)/shard_map/ppermute | solution.py:710
  110.5 24.5 %collective-permute-start.2 = (bf16[256,2048]{1,0:T(8,128)(2,1)S(1)}, bf16[256,2048]{1,0:T(8,128)(2,1)S(1)}, u32[]{:S(2)}, u32[]{:S(2)}) collective-permute-start(bf16[256,2048]{1,0:T(8,128)(2,1)S(1)} %copy-done.1), channel_id=1, source_target_pairs={{0,8},{1,9},{2,10},{3,11},{4,12},{5,13},{6,14},{7,15},{8,0},{9,1},... | collective-permute-start | bytes 3145736 | tf_op jit(solution)/shard_map/ppermute | solution.py:710
  110.5 24.4 %collective-permute-start.1 = (bf16[256,2048]{1,0:T(8,128)(2,1)S(1)}, bf16[256,2048]{1,0:T(8,128)(2,1)S(1)}, u32[]{:S(2)}, u32[]{:S(2)}) collective-permute-start(bf16[256,2048]{1,0:T(8,128)(2,1)S(1)} %copy-done.5), channel_id=1, source_target_pairs={{0,2},{1,3},{2,0},{3,1},{4,6},{5,7},{6,4},{7,5},{8,10},{9,11},{10,... | collective-permute-start | bytes 3145736 | tf_op jit(solution)/shard_map/ppermute | solution.py:710
  110.6 26.3 %collective-permute-start.3 = (bf16[256,2048]{1,0:T(8,128)(2,1)S(1)}, bf16[256,2048]{1,0:T(8,128)(2,1)}, u32[]{:S(2)}, u32[]{:S(2)}) collective-permute-start(bf16[256,2048]{1,0:T(8,128)(2,1)S(1)} %copy-done.6), channel_id=1, source_target_pairs={{0,4},{1,5},{2,6},{3,7},{4,0},{5,1},{6,2},{7,3},{8,12},{9,13},{10,... | collective-permute-start | bytes 3145736 | tf_op jit(solution)/shard_map/ppermute | solution.py:710
  135.0 1.0 copy-start.8
  135.9 1.0 copy-start.7
  216.7 104.7 %collective-permute-start.4 = (f32[256,2048]{1,0:T(8,128)}, f32[256,2048]{1,0:T(8,128)}, u32[]{:S(2)}, u32[]{:S(2)}) collective-permute-start(f32[256,2048]{1,0:T(8,128)} %get-tuple-element.64), channel_id=1, source_target_pairs={{0,2},{1,3},{2,0},{3,1},{4,6},{5,7},{6,4},{7,5},{8,10},{9,11},{10,... | collective-permute-start | bytes 6291464 | tf_op jit(solution)/shard_map/ppermute | solution.py:710
  217.1 103.6 %copy-start.10 = (f32[16,2,1024]{2,1,0:T(2,128)S(1)}, f32[16,2,1024]{2,1,0:T(2,128)}, u32[]{:S(2)}) copy-start(f32[16,2,1024]{2,1,0:T(2,128)} %get-tuple-element.71) | copy-start | bytes 393220
  217.1 104.3 %copy-start.2 = (f32[256,2048]{1,0:T(8,128)S(1)}, f32[256,2048]{1,0:T(8,128)}, u32[]{:S(2)}) copy-start(f32[256,2048]{1,0:T(8,128)} %get-tuple-element.58) | copy-start | bytes 6291460
  217.1 104.4 %copy-start.3 = (bf16[256,1024]{1,0:T(8,128)(2,1)S(1)}, bf16[256,1024]{1,0:T(8,128)(2,1)}, u32[]{:S(2)}) copy-start(bf16[256,1024]{1,0:T(8,128)(2,1)} %x_ref.3) | copy-start | bytes 1572868
  217.1 106.8 %copy-start.4 = (bf16[256,1024]{1,0:T(8,128)(2,1)S(1)}, bf16[256,1024]{1,0:T(8,128)(2,1)}, u32[]{:S(2)}) copy-start(bf16[256,1024]{1,0:T(8,128)(2,1)} %param.13) | copy-start | bytes 1572868
  217.1 106.8 %copy-start.9 = (bf16[1024,32]{0,1:T(8,128)(2,1)S(1)}, bf16[1024,32]{0,1:T(8,128)(2,1)}, u32[]{:S(2)}) copy-start(bf16[1024,32]{0,1:T(8,128)(2,1)} %param.8) | copy-start | bytes 196612
  217.1 106.8 %copy-start.11 = (bf16[32,256]{1,0:T(8,128)(2,1)S(1)}, bf16[32,256]{1,0:T(8,128)(2,1)}, u32[]{:S(2)}) copy-start(bf16[32,256]{1,0:T(8,128)(2,1)} %get-tuple-element.65) | copy-start | bytes 49156
where the time goes:
time: 327 us; the launch traced here: 326 us
  Pallas kernels  282 us (86%)
  waiting for transfers between devices  22.4 us (7%)
  local copies, waits for them, and re-layouts  10 us (3%)
  other arithmetic  8.06 us (2%)
    pallas_call x1, Pallas kernels, weight_grads(): pl.pallas_call(functools.partial(grads_kernel, n_exp=n_exp, hidden=hidden...  104 us
    pallas_call x2, Pallas kernels, sort_rows(): pl.pallas_call(functools.partial(sort_kernel, n_exp=n_exp, n_blk=n_blk, s...  47.4 us
    pallas_call x1, Pallas kernels, own_rows(): pl.pallas_call(functools.partial(own_kernel, n_exp=n_exp, hidden=hidden,...  36.3 us
    pallas_call x1, Pallas kernels, first_stage(): pl.pallas_call(functools.partial(first_kernel, n_dev=n_dev, ep_size=ep_si...  35.5 us
    pallas_call x2, Pallas kernels, combine(): pl.pallas_call(functools.partial(combine_kernel, n_exp=n_exp, hidden=hidd...  27.5 us
    ppermute x5, waiting for transfers between devices, swap(): return lax.ppermute(v, all_axes, [(d, d ^ mask) for d in range(n_dev)])  22.4 us
    pallas_call x1, Pallas kernels, router_backward(): pl.pallas_call(functools.partial(router_kernel, n_dev=n_dev, ep_size=ep_s...  17.3 us
    pallas_call x1, Pallas kernels, last_stage(): pl.pallas_call(functools.partial(last_kernel, n_dev=n_dev, ep_size=ep_siz...  14.5 us
  transfers between devices with their start and end apart: 5, of which 1 were waited for; matrix products, arithmetic and copies ran while one was open for 1% of the time, Pallas kernels for 46%

commit v1 on v0

--- a/solution.py
+++ b/solution.py
@@ -57,8 +57,9 @@
     for h in range(2):
         for k, (dst, mask) in enumerate(((b2, 2), (b4, 4), (b8, 8), (b1, 1))):
             direct.append(copy(xr_ref.at[part[h], :], dst.at[part[h], :], bsend, brecv, 4 * h + k, mask))
-            direct[-1].start()
-    z = _dot(wr_ref[...], x_ref[...], 0, 1)
+    for c in direct[:4]:
+        c.start()
+    z = _dot(wr_ref[...], x_ref[...], 1, 1)
     eid = lax.broadcasted_iota(I32, z.shape, 0)
     sel = eid == ids_ref[0:1, :]
     for j in range(1, ids_ref.shape[0]):
@@ -72,7 +73,7 @@
     out_ref[0] = own_ref[ep]
     direct[3].wait_recv()
     small = [copy(own_ref.at[peer[1]], out_ref.at[r], ssem, rsem, r, r) for r, peer in peers.items()]
-    for c in small:
+    for c in small + direct[4:]:
         c.start()
     passed = []
     for h in range(2):
@@ -88,7 +89,7 @@
 
 
 def first_stage(tokens, w_router, ids_t, xr, n_dev, ep_size):
-    local = w_router.shape[1] // ep_size
+    local = w_router.shape[0] // ep_size
     n_tok = tokens.shape[0]
     vmem = pl.BlockSpec(memory_space=pltpu.VMEM)
     hbm = pl.BlockSpec(memory_space=pl.ANY)
@@ -105,51 +106,7 @@
     )(tokens, w_router, ids_t, xr)
 
 
-def last_kernel(b6, b10, b12, b7, b11, b13, b14, b15, ssem, rsem, *, n_dev, ep_size):
-    dp, ep = lax.axis_index('dp'), lax.axis_index('ep')
-    every = _peers(dp, ep, ep_size, n_dev)
-    peers = {m: every[m] for m in (1, 2, 4, 8)}
-    _greet(peers)
-
-    def copy(src, dst, k, mask):
-        return pltpu.make_async_remote_copy(src_ref=src, dst_ref=dst, send_sem=ssem.at[k], recv_sem=rsem.at[k], device_id=peers[mask], device_id_type=MESH)
-
-    n_row = b6.shape[0]
-    c0 = n_row // 3 // GRP * GRP + GRP
-    c1 = (c0 + n_row) // 2 // GRP * GRP
-    far = []
-    for k, (src, mask, lo, hi) in enumerate(((b12, 2, 0, c0), (b10, 4, c0, c1), (b6, 8, c1, n_row))):
-        far.append(copy(src.at[pl.ds(lo, hi - lo), :], b14.at[pl.ds(lo, hi - lo), :], k, mask))
-        far[-1].start()
-    near = [copy(src, dst, 3 + k, 1) for k, (src, dst) in enumerate(((b6, b7), (b10, b11), (b12, b13)))]
-    for c in near:
-        c.start()
-    for c in far:
-        c.wait_recv()
-    end = copy(b14, b15, 6, 1)
-    end.start()
-    for c in far:
-        c.wait_send()
-    for c in near:
-        c.wait()
-    end.wait()
-
-
-def last_stage(b6, b10, b12, n_dev, ep_size):
-    hbm = pl.BlockSpec(memory_space=pl.ANY)
-    return pl.pallas_call(
-        functools.partial(last_kernel, n_dev=n_dev, ep_size=ep_size),
-        out_shape=[jax.ShapeDtypeStruct(b6.shape, BF16)] * 5,
-        in_specs=[hbm] * 3,
-        out_specs=[hbm] * 5,
-        scratch_shapes=[pltpu.SemaphoreType.DMA((7,)), pltpu.SemaphoreType.DMA((7,))],
-        compiler_params=pltpu.CompilerParams(collective_id=2, has_side_effects=True),
-        cost_estimate=pl.CostEstimate(flops=10_000_000_000, bytes_accessed=10_000_000, transcendentals=0),
-        name='last_stage',
-    )(b6, b10, b12)
-
-
-def router_kernel(dg_ref, g_ref, x_ref, dz_ref, gr_ref, all_ref, part_ref, take_ref, sem_a, sem_b, sem_c, sem_d, sem_e, sem_f, *, n_dev, ep_size):
+def router_kernel(dg_ref, g_ref, x_ref, dz_ref, out_ref, gr_ref, all_ref, part_ref, take_ref, sem_a, sem_b, sem_c, sem_d, sem_e, sem_f, *, n_dev, ep_size):
     dp, ep = lax.axis_index('dp'), lax.axis_index('ep')
     me = dp * ep_size + ep
     peers = _peers(dp, ep, ep_size, n_dev)
@@ -187,6 +144,7 @@
         copies[-1].start()
     for c in copies:
         c.wait()
+    out_ref[...] = jnp.concatenate([gr_ref[k] for k in range(n_dev)], axis=0)
 
 
 def router_backward(dg, gates, tokens, n_dev, ep_size):
@@ -197,10 +155,11 @@
     dma = pltpu.SemaphoreType.DMA((n_dev,))
     return pl.pallas_call(
         functools.partial(router_kernel, n_dev=n_dev, ep_size=ep_size),
-        out_shape=[jax.ShapeDtypeStruct((n_exp, n_tok), BF16), jax.ShapeDtypeStruct((n_dev, rows, hidden), F32)],
+        out_shape=[jax.ShapeDtypeStruct((n_exp, n_tok), BF16), jax.ShapeDtypeStruct((n_exp, hidden), F32)],
         in_specs=[vmem] * 3,
         out_specs=[vmem] * 2,
         scratch_shapes=[
+            pltpu.VMEM((n_dev, rows, hidden), F32),
             pltpu.VMEM((ep_size, n_exp // ep_size, n_tok), F32),
             pltpu.VMEM((n_dev, rows, hidden), F32),
             pltpu.VMEM((n_dev, rows, hidden), F32),
@@ -231,8 +190,9 @@
         gate_ref[rows, :] = jnp.where(eq, g_ref[at, :], 0.0)
 
 
-def sort_kernel(meta_ref, code_ref, zero_ref, g_ref, start_ref, *rest, n_exp, n_blk, skip):
+def sort_kernel(meta_ref, code_ref, zero_ref, rel_ref, g_ref, start_ref, *rest, n_exp, n_blk, more):
     srcs = rest[:n_blk]
+    rest = rest[more:]
     out_ref, slot_ref, x_ref, buf_ref, zbuf_ref, hot_ref, gate_ref, xsem, sem_ref, zsem = rest[n_blk:]
     hidden = x_ref.shape[2] // 2
 
@@ -260,12 +220,13 @@
             lax.fori_loop(0, cnt, one, 0)
 
     def block(i, c):
-        n_grp = meta_ref[skip + i]
+        rel = rel_ref[i]
+        n_grp = meta_ref[rel]
         pltpu.make_async_copy(srcs[0], x_ref.at[i], xsem.at[i]).wait()
 
         def step(k, c):
             s, old, newer = c
-            _onehot(code_ref, skip + i, k, slot_ref, g_ref, hot_ref, gate_ref, n_exp)
+            _onehot(code_ref, rel, k, slot_ref, g_ref, hot_ref, gate_ref, n_exp)
             gcol = jnp.sum(gate_ref[...], axis=1, keepdims=True)
             hot = hot_ref[...]
             drain(s, old)
@@ -274,7 +235,7 @@
             cnt = jnp.minimum(n_grp - k * PER, PER)
 
             def send(q, c):
-                code = code_ref[skip + i, k * PER + q]
+                code = code_ref[rel, k * PER + q]
                 dst = pl.multiple_of(code - lax.rem(code, GRP), GRP)
                 pltpu.make_async_copy(buf_ref.at[s, pl.ds(pl.multiple_of(q * GRP, GRP), GRP), :], out_ref.at[pl.ds(dst, GRP), :], sem_ref.at[s]).start()
                 return c
@@ -299,16 +260,19 @@
         lax.fori_loop(0, zero_ref[1, e], lambda q, c: (zeros(0).wait(), c)[1], 0)
 
 
-def sort_rows(meta, code, zero, gates, start, blocks, skip, rows, n_exp):
+def sort_rows(meta, code, zero, gates, start, blk, rels, rows, n_exp, into=None):
+    blocks = [blk[k] for k in rels]
     n_blk = len(blocks)
+    more = [] if into is None else [into]
     width = blocks[0].shape[1]
     smem = pl.BlockSpec(memory_space=pltpu.SMEM)
     vmem = pl.BlockSpec(memory_space=pltpu.VMEM)
     hbm = pl.BlockSpec(memory_space=pl.ANY)
     return pl.pallas_call(
-        functools.partial(sort_kernel, n_exp=n_exp, n_blk=n_blk, skip=skip),
+        functools.partial(sort_kernel, n_exp=n_exp, n_blk=n_blk, more=len(more)),
         out_shape=jax.ShapeDtypeStruct((rows, width), BF16),
-        in_specs=[smem] * 3 + [vmem] * 2 + [hbm] * n_blk,
+        in_specs=[smem] * 4 + [vmem] * 2 + [hbm] * (n_blk + len(more)),
+        input_output_aliases={6 + n_blk: 0} if more else {},
         out_specs=hbm,
         scratch_shapes=[
             pltpu.VMEM(gates.shape, I32),
@@ -322,7 +286,7 @@
             pltpu.SemaphoreType.DMA((1,)),
         ],
         cost_estimate=pl.CostEstimate(flops=1_500_000_000 * n_blk, bytes_accessed=3_000_000 * n_blk, transcendentals=0),
-    )(meta, code, zero, gates, start, *blocks)
+    )(meta, code, zero, jnp.array(rels, I32), gates, start, *blocks, *more)
 
 
 def _units(first, n, src_ref, buf_ref, sem, slot, op):
@@ -711,11 +675,10 @@
 
     def layer(tokens, w_router, w_gate, w_up, w_down, top_ids, r_proj):
         n_local, hidden = tokens.shape
-        n_exp = w_router.shape[1]
         local_exp = w_gate.shape[0]
         xr = jnp.concatenate([tokens, r_proj], axis=1)
         blk = {0: xr}
-        own_gates, gates, *got = first_stage(tokens, w_router, top_ids.T, xr, n_dev, ep_size)
+        own_gates, gates, *got = first_stage(tokens, w_router.T, top_ids.T, xr, n_dev, ep_size)
         blk.update(zip((1, 2, 4, 8, 3, 5, 9), got))
         for dst, src, mask in ((6, 4, 2), (12, 8, 4), (10, 2, 8)):
             blk[dst] = swap(blk[src], mask)
@@ -724,15 +687,21 @@
         meta, start, code, ta, za, tb, zb = routing_tables(cnt, ep_size)
         own_n = ep_size * n_local * local_exp + local_exp * UNIT
         oth_n = (n_dev - ep_size) * n_local * local_exp + local_exp * UNIT
-        uo = sort_rows(meta, code, za, gates, start, [blk[k] for k in range(4)], 0, own_n, local_exp)
+        uo = sort_rows(meta, code, za, gates, start, blk, (0, 1, 2, 3), own_n, local_exp)
         o_rows, sv = own_rows(ta, uo, w_gate, w_up, w_down)
+        o_rows, blk[6], blk[10], blk[12] = lax.optimization_barrier((o_rows, blk[6], blk[10], blk[12]))
+        c0, c1 = 96, 176
+        far = []
+        for v, mask in ((blk[12][:c0], 2), (blk[10][c0:c1], 4), (blk[6][c1:], 8)):
+            far.append(swap(v, mask))
+        for k in (6, 10, 12):
+            blk[k + 1] = swap(blk[k], 1)
+        ud = sort_rows(meta, code, zb, gates, start, blk, (4, 5, 8, 9, 6, 10, 12), oth_n, local_exp)
+        blk[14] = jnp.concatenate(far, axis=0)
+        blk[15] = swap(blk[14], 1)
         p_send, dg_b = combine(meta, code, gates, start, blk, o_rows, (1, 3), local_exp)
         p_sib = swap(p_send, 1)
-        late = [blk[6], blk[10], blk[12]]
-        p_send, *late = lax.optimization_barrier((p_send, *late))
-        blk[6], blk[10], blk[12] = late
-        blk[7], blk[11], blk[13], blk[14], blk[15] = last_stage(*late, n_dev, ep_size)
-        ud = sort_rows(meta, code, zb, gates, start, [blk[k] for k in range(4, 16)], 4, oth_n, local_exp)
+        ud = sort_rows(meta, code, jnp.zeros_like(zb), gates, start, blk, (7, 11, 13, 14, 15), oth_n, local_exp, ud)
         p_sib, ud = lax.optimization_barrier((p_sib, ud))
         p_keep, p_go, dg_a = combine(meta, code, gates, start, blk, o_rows, (0, 2), local_exp, p_sib)
         dg = jnp.stack([dg_a[0], dg_b[0], dg_a[1], dg_b[1]])
@@ -740,7 +709,7 @@
         p_go, dz_t = lax.optimization_barrier((p_go, dz_t))
         p_far = swap(p_go, 2)
         g_gate, g_up, g_down = weight_grads(ta, tb, uo, sv, ud, w_gate, w_up, w_down)
-        grad_router = grad_router_t.reshape(n_exp, hidden).T
+        grad_router = grad_router_t.T
         y = tokens.astype(F32) + (p_keep[:, :hidden] + p_far[:, :hidden])
         dx = r_proj.astype(F32) + _dot(dz_t, w_router, 0, 1) + (p_keep[:, hidden:] + p_far[:, hidden:])
         return y, dx, g_gate, g_up, g_down, grad_router

time: 327 us -> 311 us (0.951)
  Pallas kernels: 282 us -> 270 us
  waiting for transfers between devices: 22.4 us -> 13.8 us
  starting transfers between devices: 0.54 us -> 6.49 us
    pallas_call x3, Pallas kernels: 61.8 us -> 50 us  [sort_rows(): pl.pallas_call(functools.partial(sort_kernel, n_exp=n_exp, n_blk=n_blk, m...]
    ppermute x5 -> x12, waiting for transfers between devices: 22.4 us -> 13.8 us  [swap(): return lax.ppermute(v, all_axes, [(d, d ^ mask) for d in range(n_dev)])]
    ppermute x5 -> x12, starting transfers between devices: 0.54 us -> 6.49 us  [swap(): return lax.ppermute(v, all_axes, [(d, d ^ mask) for d in range(n_dev)])]
  transfers between devices with their start and end apart: 5 -> 12, of which waited for: 1 -> 2; matrix products, arithmetic and copies ran while one was open for 1% -> 3% of each run, Pallas kernels for 46% -> 61%
where the time goes in v1:
time: 311 us
  Pallas kernels  270 us (87%)
  waiting for transfers between devices  13.8 us (4%)
  local copies, waits for them, and re-layouts  8.49 us (3%)
  other arithmetic  8.03 us (3%)
  starting transfers between devices  6.49 us (2%)
    pallas_call x1, Pallas kernels, weight_grads(): pl.pallas_call(functools.partial(grads_kernel, n_exp=n_exp, hidden=hidden...  104 us
    pallas_call x3, Pallas kernels, sort_rows(): pl.pallas_call(functools.partial(sort_kernel, n_exp=n_exp, n_blk=n_blk, m...  50 us
    pallas_call x1, Pallas kernels, own_rows(): pl.pallas_call(functools.partial(own_kernel, n_exp=n_exp, hidden=hidden,...  36.3 us
    pallas_call x1, Pallas kernels, first_stage(): pl.pallas_call(functools.partial(first_kernel, n_dev=n_dev, ep_size=ep_si...  36.3 us
    pallas_call x2, Pallas kernels, combine(): pl.pallas_call(functools.partial(combine_kernel, n_exp=n_exp, hidden=hidd...  27.3 us
    pallas_call x1, Pallas kernels, router_backward(): pl.pallas_call(functools.partial(router_kernel, n_dev=n_dev, ep_size=ep_s...  16.7 us
    ppermute x12, waiting for transfers between devices, swap(): return lax.ppermute(v, all_axes, [(d, d ^ mask) for d in range(n_dev)])  13.8 us
    ppermute x12, starting transfers between devices, swap(): return lax.ppermute(v, all_axes, [(d, d ^ mask) for d in range(n_dev)])  6.49 us
  transfers between devices with their start and end apart: 12, of which 2 were waited for; matrix products, arithmetic and copies ran while one was open for 3% of the time, Pallas kernels for 61%

profile of v1, /device:TPU:1, one launch (start us, length us, event | category | flops | bytes accessed | tf_op | source)
XLA Modules:
  0.0 310.5 jit_solution(5108974597960695545)
XLA Ops:
  0.6 1.1 constant_dynamic-update-slice_fusion.1
  1.7 1.1 constant_dynamic-update-slice_fusion.xr_ref.rest_0_.r_ref_a
  2.8 1.0 copy-done
  3.8 36.3 %first_stage.1 = (f32[4,8,256]{2,1,0:T(8,128)}, f32[16,8,256]{2,1,0:T(8,128)}, bf16[256,2048]{1,0:T(8,128)(2,1)}, bf16[256,2048]{1,0:T(8,128)(2,1)}, bf16[256,20...) custom-call(bf16[256,1024]{1,0:T(8,128)(2,1)} %x_ref.3, ...), custom_call_target="tpu_custom_call" | custom-call | flops 20000000000 | bytes 20000000 | tf_op jit(solution)/shard_map/first_stage/pallas_call | solution.py:97
  40.4 1.2 collective-permute-start
  41.8 1.3 convert_reduce_fusion
  44.7 0.7 select_reduce_fusion.code_ref
  46.0 0.7 broadcast_in_dim.36.start_ref
  47.2 14.1 %shard_map.145.ud_ref.uo_ref = bf16[9216,2048]{1,0:T(8,128)(2,1)} custom-call(s32[16]{0:T(128)} %and_select_fusion.8.meta_ref, s32[16,128]{1,0:T(8,128)} %select_reduce_fusion.code_ref, s32[2,8]{1,0:T(2,128)} %get-tuple-element.79.zero_ref, s32[4]{0:T(128)} %call_exported.0.rel_ref, f32[128,256]{1,0:T(8,128)} %bitcast.38, ...), custom_call_target="tpu_custom_call" | custom-call | flops 6000000000 | bytes 12000000 | tf_op jit(solution)/shard_map/pallas_call | solution.py:271
  61.4 36.3 %own_rows.1 = (bf16[9216,2048]{1,0:T(8,128)(2,1)}, bf16[9216,1536]{1,0:T(8,128)(2,1)}) custom-call(s32[2,8]{1,0:T(2,128)} %get-tuple-element.78.t_ref.ta_ref, bf16[9216,2048]{1,0:T(8,128)(2,1)} %shard_map.145.ud_ref.uo_ref, bf16[8,1024,512]{2,1,0:T(8,128)(2,1)} %w1_ref.3, bf16[8,1024,512]{2,1,0:T(8,128)(2,1)} %w3_ref.3, bf16[8,512,1024]{2,1,0:T(8,128)(2,1)} %w2_ref.3), custom_call_target="tpu_custom_call" | custom-call | flops 30000001024 | bytes 60000000 | tf_op jit(solution)/shard_map/own_rows/pallas_call | solution.py:406
  97.7 13.9 %combine.2 = (f32[512,2048]{1,0:T(8,128)}, f32[2,8,256]{2,1,0:T(8,128)}) custom-call(s32[16]{0:T(128)} %and_select_fusion.8.meta_ref, s32[16,128]{1,0:T(8,128)} %select_reduce_fusion.code_ref, f32[128,256]{1,0:T(8,128)} %bitcast.39, s32[128,256]{1,0:T(8,128)} %broadcast_in_dim.36.start_ref, bf16[256,2048]{1,0:T(8,128)(2,1)} %get-tuple-element.37.rest_1_.r_ref_a, ...), custom_call_target="tpu_custom_call" | custom-call | flops 8000000000 | bytes 20000000 | tf_op jit(solution)/shard_map/combine/pallas_call | solution.py:629
  113.0 1.0 slice.43
  114.6 7.3 %collective-permute-done.7 = bf16[96,2048]{1,0:T(8,128)(2,1)S(1)} collective-permute-done((bf16[96,2048]{1,0:T(8,128)(2,1)S(1)}, bf16[96,2048]{1,0:T(8,128)(2,1)S(1)}, u32[]{:S(2)}, u32[]{:S(2)}) %collective-permute-start.7) | collective-permute-done | bytes 393248 | tf_op jit(solution)/shard_map/ppermute | solution.py:674
  122.0 1.4 collective-permute-start.6
  123.4 6.5 %collective-permute-done.9 = bf16[80,2048]{1,0:T(8,128)(2,1)S(1)} collective-permute-done((bf16[80,2048]{1,0:T(8,128)(2,1)S(1)}, bf16[80,2048]{1,0:T(8,128)(2,1)S(1)}, u32[]{:S(2)}, u32[]{:S(2)}) %collective-permute-start.9) | collective-permute-done | bytes 327712 | tf_op jit(solution)/shard_map/ppermute | solution.py:674
  129.9 2.2 collective-permute-start.10
  132.8 21.2 %shard_map.146.rest_5_ = bf16[25600,2048]{1,0:T(8,128)(2,1)} custom-call(s32[16]{0:T(128)} %and_select_fusion.8.meta_ref, s32[16,128]{1,0:T(8,128)} %select_reduce_fusion.code_ref, s32[2,8]{1,0:T(2,128)} %pad_add_fusion.2.zero_ref, s32[7]{0:T(128)} %constant.104.clone.rel_ref, f32[128,256]{1,0:T(8,128)} %bitcast.40, s32[128,256]{1,0:T(8,128)} %broadcast_in_dim.36.start_ref, ...), custom_call_target="tpu_custom_call" | custom-call | flops 10499999744 | bytes 21000000 | tf_op jit(solution)/shard_map/pallas_call | solution.py:271
  154.7 14.7 %shard_map.147.ud_ref = bf16[25600,2048]{1,0:T(8,128)(2,1)} custom-call(s32[16]{0:T(128)} %and_select_fusion.8.meta_ref, s32[16,128]{1,0:T(8,128)} %select_reduce_fusion.code_ref, s32[2,8]{1,0:T(2,128)} %broadcast_14_zero_ref.2.zero_ref, s32[5]{0:T(128)} %constant.105.clone.rel_ref, f32[128,256]{1,0:T(8,128)} %bitcast.41, ...), custom_call_target="tpu_custom_call", output_to_operand_aliasing={{}: (11, {})} | custom-call | flops 7500000256 | bytes 15000000 | tf_op jit(solution)/shard_map/pallas_call | solution.py:271
  169.4 13.4 %combine.3 = (f32[256,2048]{1,0:T(8,128)}, f32[256,2048]{1,0:T(8,128)}, f32[2,8,256]{2,1,0:T(8,128)}) custom-call(s32[16]{0:T(128)} %and_select_fusion.8.meta_ref, s32[16,128]{1,0:T(8,128)} %select_reduce_fusion.code_ref, f32[128,256]{1,0:T(8,128)} %bitcast.42, s32[128,256]{1,0:T(8,128)} %broadcast_in_dim.36.start_ref, bf16[256,2048]{1,0:T(8,128)(2,1)} %copy-done, ...), custom_call_target="tpu_custom_call" | custom-call | flops 8000000000 | bytes 20000000 | tf_op jit(solution)/shard_map/combine/pallas_call | solution.py:629
  182.8 0.7 fusion.14
  184.2 16.7 %router_backward.1 = (bf16[32,256]{1,0:T(8,128)(2,1)}, f32[32,1024]{1,0:T(8,128)}) custom-call(f32[4,8,256]{2,1,0:T(8,128)} %pad_maximum_fusion.dg_ref, f32[4,8,256]{2,1,0:T(8,128)} %get-tuple-element.54.g_ref, bf16[256,1024]{1,0:T(8,128)(2,1)} %x_ref.3), custom_call_target="tpu_custom_call" | custom-call | flops 2000000000 | bytes 2000000 | tf_op jit(solution)/shard_map/router_backward/pallas_call | solution.py:156
  201.3 103.5 %weight_grads.1 = (f32[8,1024,512]{2,1,0:T(8,128)}, f32[8,1024,512]{2,1,0:T(8,128)}, f32[8,512,1024]{2,1,0:T(8,128)}) custom-call(s32[2,8]{1,0:T(2,128)} %get-tuple-element.78.t_ref.ta_ref, s32[2,8]{1,0:T(2,128)} %pad_add_fusion.3.tb_ref, bf16[9216,2048]{1,0:T(8,128)(2,1)} %shard_map.145.ud_ref.uo_ref, bf16[9216,1536]{1,0:T(8,128)(2,1)} %get-tuple-element.58.sv_ref, ...), custom_call_target="tpu_custom_call" | custom-call | flops 89999998976 | bytes 150000000 | tf_op jit(solution)/shard_map/weight_grads/pallas_call | solution.py:509
  304.9 2.4 fusion.1
  307.3 2.5 fusion
  (74 shorter events, 8.3 us)
Async XLA Ops:
  2.8 1.0 copy-start
  40.0 57.6 %collective-permute-start.1 = (bf16[256,2048]{1,0:T(8,128)(2,1)}, bf16[256,2048]{1,0:T(8,128)(2,1)S(1)}, u32[]{:S(2)}, u32[]{:S(2)}) collective-permute-start(bf16[256,2048]{1,0:T(8,128)(2,1)} %get-tuple-element.36.rest_2_.r_ref_b), channel_id=1, source_target_pairs={{0,8},{1,9},{2,10},{3,11},{4,12},{5,13},{6,14},{7,15},{8,0},{9,1},... | collective-permute-start | bytes 3145736 | tf_op jit(solution)/shard_map/ppermute | solution.py:674
  40.4 57.3 %collective-permute-start = (bf16[256,2048]{1,0:T(8,128)(2,1)}, bf16[256,2048]{1,0:T(8,128)(2,1)}, u32[]{:S(2)}, u32[]{:S(2)}) collective-permute-start(bf16[256,2048]{1,0:T(8,128)(2,1)} %get-tuple-element.40.rest_0_), channel_id=1, source_target_pairs={{0,2},{1,3},{2,0},{3,1},{4,6},{5,7},{6,4},{7,5},{8,10},{9,11},{10,... | collective-permute-start | bytes 3145736 | tf_op jit(solution)/shard_map/ppermute | solution.py:674
  41.5 56.2 %collective-permute-start.2 = (bf16[256,2048]{1,0:T(8,128)(2,1)}, bf16[256,2048]{1,0:T(8,128)(2,1)S(1)}, u32[]{:S(2)}, u32[]{:S(2)}) collective-permute-start(bf16[256,2048]{1,0:T(8,128)(2,1)} %get-tuple-element.41.rest_2_), channel_id=1, source_target_pairs={{0,4},{1,5},{2,6},{3,7},{4,0},{5,1},{6,2},{7,3},{8,12},{9,13},{10,... | collective-permute-start | bytes 3145736 | tf_op jit(solution)/shard_map/ppermute | solution.py:674
  97.7 16.9 %copy-start.6 = (bf16[256,2048]{1,0:T(8,128)(2,1)}, bf16[256,2048]{1,0:T(8,128)(2,1)S(1)}, u32[]{:S(2)}) copy-start(bf16[256,2048]{1,0:T(8,128)(2,1)S(1)} %collective-permute-done.1.rest_5_) | copy-start | bytes 3145732
  97.7 24.3 %copy-start.4 = (bf16[256,2048]{1,0:T(8,128)(2,1)}, bf16[256,2048]{1,0:T(8,128)(2,1)S(1)}, u32[]{:S(2)}) copy-start(bf16[256,2048]{1,0:T(8,128)(2,1)S(1)} %collective-permute-done.2.rest_6_) | copy-start | bytes 3145732
  111.6 57.8 %collective-permute-start.3 = (f32[512,2048]{1,0:T(8,128)}, f32[512,2048]{1,0:T(8,128)}, u32[]{:S(2)}, u32[]{:S(2)}) collective-permute-start(f32[512,2048]{1,0:T(8,128)} %get-tuple-element.43), channel_id=1, source_target_pairs={{0,1},{1,0},{2,3},{3,2},{4,5},{5,4},{6,7},{7,6},{8,9},{9,8},{10,11... | collective-permute-start | bytes 12582920 | tf_op jit(solution)/shard_map/ppermute | solution.py:674
  111.7 10.2 %collective-permute-start.7 = (bf16[96,2048]{1,0:T(8,128)(2,1)S(1)}, bf16[96,2048]{1,0:T(8,128)(2,1)S(1)}, u32[]{:S(2)}, u32[]{:S(2)}) collective-permute-start(bf16[96,2048]{1,0:T(8,128)(2,1)S(1)} %slice.41), channel_id=1, source_target_pairs={{0,2},{1,3},{2,0},{3,1},{4,6},{5,7},{6,4},{7,5},{8,10},{9,11},{10,... | collective-permute-start | bytes 1179656 | tf_op jit(solution)/shard_map/ppermute | solution.py:674
  112.4 9.6 %collective-permute-start.8 = (bf16[80,2048]{1,0:T(8,128)(2,1)S(1)}, bf16[80,2048]{1,0:T(8,128)(2,1)S(1)}, u32[]{:S(2)}, u32[]{:S(2)}) collective-permute-start(bf16[80,2048]{1,0:T(8,128)(2,1)S(1)} %slice.42), channel_id=1, source_target_pairs={{0,4},{1,5},{2,6},{3,7},{4,0},{5,1},{6,2},{7,3},{8,12},{9,13},{10,... | collective-permute-start | bytes 983048 | tf_op jit(solution)/shard_map/ppermute | solution.py:674
  114.0 40.0 %collective-permute-start.4 = (bf16[256,2048]{1,0:T(8,128)(2,1)}, bf16[256,2048]{1,0:T(8,128)(2,1)}, u32[]{:S(2)}, u32[]{:S(2)}) collective-permute-start(bf16[256,2048]{1,0:T(8,128)(2,1)} %collective-permute-done.rest_4_), channel_id=1, source_target_pairs={{0,1},{1,0},{2,3},{3,2},{4,5},{5,4},{6,7},{7,6},{8,9},{9,8},{10,11... | collective-permute-start | bytes 3145736 | tf_op jit(solution)/shard_map/ppermute | solution.py:674
  114.5 39.5 %collective-permute-start.5 = (bf16[256,2048]{1,0:T(8,128)(2,1)S(1)}, bf16[256,2048]{1,0:T(8,128)(2,1)}, u32[]{:S(2)}, u32[]{:S(2)}) collective-permute-start(bf16[256,2048]{1,0:T(8,128)(2,1)S(1)} %collective-permute-done.1.rest_5_), channel_id=1, source_target_pairs={{0,1},{1,0},{2,3},{3,2},{4,5},{5,4},{6,7},{7,6},{8,9},{9,8},{10,11... | collective-permute-start | bytes 3145736 | tf_op jit(solution)/shard_map/ppermute | solution.py:674
  121.9 7.9 %collective-permute-start.9 = (bf16[80,2048]{1,0:T(8,128)(2,1)S(1)}, bf16[80,2048]{1,0:T(8,128)(2,1)S(1)}, u32[]{:S(2)}, u32[]{:S(2)}) collective-permute-start(bf16[80,2048]{1,0:T(8,128)(2,1)S(1)} %slice.43), channel_id=1, source_target_pairs={{0,8},{1,9},{2,10},{3,11},{4,12},{5,13},{6,14},{7,15},{8,0},{9,1},... | collective-permute-start | bytes 983048 | tf_op jit(solution)/shard_map/ppermute | solution.py:674
  122.0 32.1 %collective-permute-start.6 = (bf16[256,2048]{1,0:T(8,128)(2,1)S(1)}, bf16[256,2048]{1,0:T(8,128)(2,1)}, u32[]{:S(2)}, u32[]{:S(2)}) collective-permute-start(bf16[256,2048]{1,0:T(8,128)(2,1)S(1)} %collective-permute-done.2.rest_6_), channel_id=1, source_target_pairs={{0,1},{1,0},{2,3},{3,2},{4,5},{5,4},{6,7},{7,6},{8,9},{9,8},{10,11... | collective-permute-start | bytes 3145736 | tf_op jit(solution)/shard_map/ppermute | solution.py:674
  129.9 24.2 %copy-start.5 = (bf16[256,2048]{1,0:T(8,128)(2,1)}, bf16[256,2048]{1,0:T(8,128)(2,1)S(1)}, u32[]{:S(2)}) copy-start(bf16[256,2048]{1,0:T(8,128)(2,1)S(1)} %constant_dynamic-update-slice_fusion.2.rest_3_) | copy-start | bytes 3145732
  129.9 24.2 %collective-permute-start.10 = (bf16[256,2048]{1,0:T(8,128)(2,1)S(1)}, bf16[256,2048]{1,0:T(8,128)(2,1)}, u32[]{:S(2)}, u32[]{:S(2)}) collective-permute-start(bf16[256,2048]{1,0:T(8,128)(2,1)S(1)} %constant_dynamic-update-slice_fusion.2.rest_3_), channel_id=1, source_target_pairs={{0,1},{1,0},{2,3},{3,2},{4,5},{5,4},{6,7},{7,6},{8,9},{9,8},{10,11... | collective-permute-start | bytes 3145736 | tf_op jit(solution)/shard_map/ppermute | solution.py:674
  200.9 104.0 %collective-permute-start.11 = (f32[256,2048]{1,0:T(8,128)}, f32[256,2048]{1,0:T(8,128)}, u32[]{:S(2)}, u32[]{:S(2)}) collective-permute-start(f32[256,2048]{1,0:T(8,128)} %get-tuple-element.56), channel_id=1, source_target_pairs={{0,2},{1,3},{2,0},{3,1},{4,6},{5,7},{6,4},{7,5},{8,10},{9,11},{10,... | collective-permute-start | bytes 6291464 | tf_op jit(solution)/shard_map/ppermute | solution.py:674
  201.3 103.6 %copy-start.1 = (f32[256,2048]{1,0:T(8,128)S(1)}, f32[256,2048]{1,0:T(8,128)}, u32[]{:S(2)}) copy-start(f32[256,2048]{1,0:T(8,128)} %get-tuple-element.50) | copy-start | bytes 6291460
  201.3 103.6 %copy-start.2 = (bf16[256,1024]{1,0:T(8,128)(2,1)S(1)}, bf16[256,1024]{1,0:T(8,128)(2,1)}, u32[]{:S(2)}) copy-start(bf16[256,1024]{1,0:T(8,128)(2,1)} %x_ref.3) | copy-start | bytes 1572868
  201.3 106.0 %copy-start.3 = (bf16[256,1024]{1,0:T(8,128)(2,1)S(1)}, bf16[256,1024]{1,0:T(8,128)(2,1)}, u32[]{:S(2)}) copy-start(bf16[256,1024]{1,0:T(8,128)(2,1)} %param.16) | copy-start | bytes 1572868
  201.3 106.1 %copy-start.8 = (bf16[1024,32]{0,1:T(8,128)(2,1)S(1)}, bf16[1024,32]{0,1:T(8,128)(2,1)}, u32[]{:S(2)}) copy-start(bf16[1024,32]{0,1:T(8,128)(2,1)} %param.11) | copy-start | bytes 196612
  201.3 106.0 %copy-start.9 = (bf16[32,256]{1,0:T(8,128)(2,1)S(1)}, bf16[32,256]{1,0:T(8,128)(2,1)}, u32[]{:S(2)}) copy-start(bf16[32,256]{1,0:T(8,128)(2,1)} %get-tuple-element.57) | copy-start | bytes 49156
  201.3 108.6 %copy-start.7 = (f32[32,1024]{1,0:T(8,128)S(1)}, f32[32,1024]{1,0:T(8,128)}, u32[]{:S(2)}) copy-start(f32[32,1024]{1,0:T(8,128)} %get-tuple-element.63) | copy-start | bytes 393220

commit v2 on v1

--- a/solution.py
+++ b/solution.py
@@ -690,16 +690,12 @@
         uo = sort_rows(meta, code, za, gates, start, blk, (0, 1, 2, 3), own_n, local_exp)
         o_rows, sv = own_rows(ta, uo, w_gate, w_up, w_down)
         o_rows, blk[6], blk[10], blk[12] = lax.optimization_barrier((o_rows, blk[6], blk[10], blk[12]))
-        c0, c1 = 96, 176
-        far = []
-        for v, mask in ((blk[12][:c0], 2), (blk[10][c0:c1], 4), (blk[6][c1:], 8)):
-            far.append(swap(v, mask))
+        blk[14] = swap(blk[12], 2)
         for k in (6, 10, 12):
             blk[k + 1] = swap(blk[k], 1)
         ud = sort_rows(meta, code, zb, gates, start, blk, (4, 5, 8, 9, 6, 10, 12), oth_n, local_exp)
-        blk[14] = jnp.concatenate(far, axis=0)
+        p_send, dg_b = combine(meta, code, gates, start, blk, o_rows, (1, 3), local_exp)
         blk[15] = swap(blk[14], 1)
-        p_send, dg_b = combine(meta, code, gates, start, blk, o_rows, (1, 3), local_exp)
         p_sib = swap(p_send, 1)
         ud = sort_rows(meta, code, jnp.zeros_like(zb), gates, start, blk, (7, 11, 13, 14, 15), oth_n, local_exp, ud)
         p_sib, ud = lax.optimization_barrier((p_sib, ud))

time: 311 us -> 315 us (1.013)
  waiting for transfers between devices: 13.8 us -> 22.2 us
    ppermute x12 -> x10, waiting for transfers between devices: 13.8 us -> 22.2 us  [swap(): return lax.ppermute(v, all_axes, [(d, d ^ mask) for d in range(n_dev)])]
    ppermute x12 -> x10, starting transfers between devices: 6.49 us -> 4.51 us  [swap(): return lax.ppermute(v, all_axes, [(d, d ^ mask) for d in range(n_dev)])]
  transfers between devices with their start and end apart: 12 -> 10, of which waited for: 2 -> 1; matrix products, arithmetic and copies ran while one was open for 3% -> 2% of each run, Pallas kernels for 61% -> 60%
where the time goes in v2:
time: 315 us
  Pallas kernels  269 us (85%)
  waiting for transfers between devices  22.2 us (7%)
  other arithmetic  8.01 us (3%)
  local copies, waits for them, and re-layouts  7.37 us (2%)
  starting transfers between devices  4.51 us (1%)
    pallas_call x1, Pallas kernels, weight_grads(): pl.pallas_call(functools.partial(grads_kernel, n_exp=n_exp, hidden=hidden...  104 us
    pallas_call x3, Pallas kernels, sort_rows(): pl.pallas_call(functools.partial(sort_kernel, n_exp=n_exp, n_blk=n_blk, m...  50.1 us
    pallas_call x1, Pallas kernels, own_rows(): pl.pallas_call(functools.partial(own_kernel, n_exp=n_exp, hidden=hidden,...  36.3 us
    pallas_call x1, Pallas kernels, first_stage(): pl.pallas_call(functools.partial(first_kernel, n_dev=n_dev, ep_size=ep_si...  36.3 us
    pallas_call x2, Pallas kernels, combine(): pl.pallas_call(functools.partial(combine_kernel, n_exp=n_exp, hidden=hidd...  27.5 us
    ppermute x10, waiting for transfers between devices, swap(): return lax.ppermute(v, all_axes, [(d, d ^ mask) for d in range(n_dev)])  22.2 us
    pallas_call x1, Pallas kernels, router_backward(): pl.pallas_call(functools.partial(router_kernel, n_dev=n_dev, ep_size=ep_s...  15.3 us
  transfers between devices with their start and end apart: 10, of which 1 were waited for; matrix products, arithmetic and copies ran while one was open for 2% of the time, Pallas kernels for 60%

profile of v2, /device:TPU:1, one launch (start us, length us, event | category | flops | bytes accessed | tf_op | source)
XLA Modules:
  0.0 314.6 jit_solution(6338754768939138124)
XLA Ops:
  0.6 1.1 constant_dynamic-update-slice_fusion.1
  1.7 1.1 constant_dynamic-update-slice_fusion.xr_ref.rest_0_.r_ref_a
  2.8 1.0 copy-done
  3.8 36.3 %first_stage.1 = (f32[4,8,256]{2,1,0:T(8,128)}, f32[16,8,256]{2,1,0:T(8,128)}, bf16[256,2048]{1,0:T(8,128)(2,1)}, bf16[256,2048]{1,0:T(8,128)(2,1)}, bf16[256,20...) custom-call(bf16[256,1024]{1,0:T(8,128)(2,1)} %x_ref.3, ...), custom_call_target="tpu_custom_call" | custom-call | flops 20000000000 | bytes 20000000 | tf_op jit(solution)/shard_map/first_stage/pallas_call | solution.py:97
  40.4 1.2 collective-permute-start
  41.8 1.3 convert_reduce_fusion
  44.7 0.7 select_reduce_fusion.code_ref
  46.0 0.7 broadcast_in_dim.36.start_ref
  47.2 14.2 %shard_map.145.ud_ref.uo_ref = bf16[9216,2048]{1,0:T(8,128)(2,1)} custom-call(s32[16]{0:T(128)} %and_select_fusion.8.meta_ref, s32[16,128]{1,0:T(8,128)} %select_reduce_fusion.code_ref, s32[2,8]{1,0:T(2,128)} %get-tuple-element.79.zero_ref, s32[4]{0:T(128)} %call_exported.0.rel_ref, f32[128,256]{1,0:T(8,128)} %bitcast.38, ...), custom_call_target="tpu_custom_call" | custom-call | flops 6000000000 | bytes 12000000 | tf_op jit(solution)/shard_map/pallas_call | solution.py:271
  61.4 36.3 %own_rows.1 = (bf16[9216,2048]{1,0:T(8,128)(2,1)}, bf16[9216,1536]{1,0:T(8,128)(2,1)}) custom-call(s32[2,8]{1,0:T(2,128)} %get-tuple-element.78.t_ref.ta_ref, bf16[9216,2048]{1,0:T(8,128)(2,1)} %shard_map.145.ud_ref.uo_ref, bf16[8,1024,512]{2,1,0:T(8,128)(2,1)} %w1_ref.3, bf16[8,1024,512]{2,1,0:T(8,128)(2,1)} %w3_ref.3, bf16[8,512,1024]{2,1,0:T(8,128)(2,1)} %w2_ref.3), custom_call_target="tpu_custom_call" | custom-call | flops 30000001024 | bytes 60000000 | tf_op jit(solution)/shard_map/own_rows/pallas_call | solution.py:406
  97.8 14.1 %combine.2 = (f32[512,2048]{1,0:T(8,128)}, f32[2,8,256]{2,1,0:T(8,128)}) custom-call(s32[16]{0:T(128)} %and_select_fusion.8.meta_ref, s32[16,128]{1,0:T(8,128)} %select_reduce_fusion.code_ref, f32[128,256]{1,0:T(8,128)} %bitcast.39, s32[128,256]{1,0:T(8,128)} %broadcast_in_dim.36.start_ref, bf16[256,2048]{1,0:T(8,128)(2,1)} %get-tuple-element.37.rest_1_.r_ref_a, ...), custom_call_target="tpu_custom_call" | custom-call | flops 8000000000 | bytes 20000000 | tf_op jit(solution)/shard_map/combine/pallas_call | solution.py:629
  114.1 22.2 %collective-permute-done.7.rest_3_ = bf16[256,2048]{1,0:T(8,128)(2,1)} collective-permute-done((bf16[256,2048]{1,0:T(8,128)(2,1)S(1)}, bf16[256,2048]{1,0:T(8,128)(2,1)}, u32[]{:S(2)}, u32[]{:S(2)}) %collective-permute-start.7) | collective-permute-done | bytes 1048608 | tf_op jit(solution)/shard_map/ppermute | solution.py:674
  136.3 1.3 collective-permute-start.8
  137.7 0.7 fusion.15
  138.4 21.2 %shard_map.146.rest_5_ = bf16[25600,2048]{1,0:T(8,128)(2,1)} custom-call(s32[16]{0:T(128)} %and_select_fusion.8.meta_ref, s32[16,128]{1,0:T(8,128)} %select_reduce_fusion.code_ref, s32[2,8]{1,0:T(2,128)} %pad_add_fusion.2.zero_ref, s32[7]{0:T(128)} %constant.104.clone.rel_ref, f32[128,256]{1,0:T(8,128)} %bitcast.40, s32[128,256]{1,0:T(8,128)} %broadcast_in_dim.36.start_ref, ...), custom_call_target="tpu_custom_call" | custom-call | flops 10499999744 | bytes 21000000 | tf_op jit(solution)/shard_map/pallas_call | solution.py:271
  160.2 14.7 %shard_map.147.ud_ref = bf16[25600,2048]{1,0:T(8,128)(2,1)} custom-call(s32[16]{0:T(128)} %and_select_fusion.8.meta_ref, s32[16,128]{1,0:T(8,128)} %select_reduce_fusion.code_ref, s32[2,8]{1,0:T(2,128)} %broadcast_14_zero_ref.2.zero_ref, s32[5]{0:T(128)} %constant.105.clone.rel_ref, f32[128,256]{1,0:T(8,128)} %bitcast.41, ...), custom_call_target="tpu_custom_call", output_to_operand_aliasing={{}: (11, {})} | custom-call | flops 7500000256 | bytes 15000000 | tf_op jit(solution)/shard_map/pallas_call | solution.py:271
  174.9 13.4 %combine.3 = (f32[256,2048]{1,0:T(8,128)}, f32[256,2048]{1,0:T(8,128)}, f32[2,8,256]{2,1,0:T(8,128)}) custom-call(s32[16]{0:T(128)} %and_select_fusion.8.meta_ref, s32[16,128]{1,0:T(8,128)} %select_reduce_fusion.code_ref, f32[128,256]{1,0:T(8,128)} %bitcast.42, s32[128,256]{1,0:T(8,128)} %broadcast_in_dim.36.start_ref, bf16[256,2048]{1,0:T(8,128)(2,1)} %copy-done, ...), custom_call_target="tpu_custom_call" | custom-call | flops 8000000000 | bytes 20000000 | tf_op jit(solution)/shard_map/combine/pallas_call | solution.py:629
  188.4 0.7 fusion.14
  189.1 0.6 pad_maximum_fusion.dg_ref
  189.7 15.3 %router_backward.1 = (bf16[32,256]{1,0:T(8,128)(2,1)}, f32[32,1024]{1,0:T(8,128)}) custom-call(f32[4,8,256]{2,1,0:T(8,128)} %pad_maximum_fusion.dg_ref, f32[4,8,256]{2,1,0:T(8,128)} %get-tuple-element.54.g_ref, bf16[256,1024]{1,0:T(8,128)(2,1)} %x_ref.3), custom_call_target="tpu_custom_call" | custom-call | flops 2000000000 | bytes 2000000 | tf_op jit(solution)/shard_map/router_backward/pallas_call | solution.py:156
  205.4 103.5 %weight_grads.1 = (f32[8,1024,512]{2,1,0:T(8,128)}, f32[8,1024,512]{2,1,0:T(8,128)}, f32[8,512,1024]{2,1,0:T(8,128)}) custom-call(s32[2,8]{1,0:T(2,128)} %get-tuple-element.78.t_ref.ta_ref, s32[2,8]{1,0:T(2,128)} %pad_add_fusion.3.tb_ref, bf16[9216,2048]{1,0:T(8,128)(2,1)} %shard_map.145.ud_ref.uo_ref, bf16[9216,1536]{1,0:T(8,128)(2,1)} %get-tuple-element.58.sv_ref, ...), custom_call_target="tpu_custom_call" | custom-call | flops 89999998976 | bytes 150000000 | tf_op jit(solution)/shard_map/weight_grads/pallas_call | solution.py:509
  309.0 2.4 fusion.1
  311.4 2.5 fusion
  313.9 0.7 copy.30
  (64 shorter events, 6.4 us)
Async XLA Ops:
  2.8 1.0 copy-start
  40.0 57.7 %collective-permute-start.1 = (bf16[256,2048]{1,0:T(8,128)(2,1)}, bf16[256,2048]{1,0:T(8,128)(2,1)S(1)}, u32[]{:S(2)}, u32[]{:S(2)}) collective-permute-start(bf16[256,2048]{1,0:T(8,128)(2,1)} %get-tuple-element.36.rest_2_.r_ref_b), channel_id=1, source_target_pairs={{0,8},{1,9},{2,10},{3,11},{4,12},{5,13},{6,14},{7,15},{8,0},{9,1},... | collective-permute-start | bytes 3145736 | tf_op jit(solution)/shard_map/ppermute | solution.py:674
  40.4 57.4 %collective-permute-start = (bf16[256,2048]{1,0:T(8,128)(2,1)}, bf16[256,2048]{1,0:T(8,128)(2,1)S(1)}, u32[]{:S(2)}, u32[]{:S(2)}) collective-permute-start(bf16[256,2048]{1,0:T(8,128)(2,1)} %get-tuple-element.40.rest_0_), channel_id=1, source_target_pairs={{0,2},{1,3},{2,0},{3,1},{4,6},{5,7},{6,4},{7,5},{8,10},{9,11},{10,... | collective-permute-start | bytes 3145736 | tf_op jit(solution)/shard_map/ppermute | solution.py:674
  41.5 56.3 %collective-permute-start.2 = (bf16[256,2048]{1,0:T(8,128)(2,1)}, bf16[256,2048]{1,0:T(8,128)(2,1)S(1)}, u32[]{:S(2)}, u32[]{:S(2)}) collective-permute-start(bf16[256,2048]{1,0:T(8,128)(2,1)} %get-tuple-element.41.rest_2_), channel_id=1, source_target_pairs={{0,4},{1,5},{2,6},{3,7},{4,0},{5,1},{6,2},{7,3},{8,12},{9,13},{10,... | collective-permute-start | bytes 3145736 | tf_op jit(solution)/shard_map/ppermute | solution.py:674
  97.8 15.9 %copy-start.4 = (bf16[256,2048]{1,0:T(8,128)(2,1)}, bf16[256,2048]{1,0:T(8,128)(2,1)S(1)}, u32[]{:S(2)}) copy-start(bf16[256,2048]{1,0:T(8,128)(2,1)S(1)} %collective-permute-done.1.rest_5_) | copy-start | bytes 3145732
  97.8 15.8 %copy-start.6 = (bf16[256,2048]{1,0:T(8,128)(2,1)}, bf16[256,2048]{1,0:T(8,128)(2,1)S(1)}, u32[]{:S(2)}) copy-start(bf16[256,2048]{1,0:T(8,128)(2,1)S(1)} %collective-permute-done.rest_4_) | copy-start | bytes 3145732
  97.8 15.3 %copy-start.5 = (bf16[256,2048]{1,0:T(8,128)(2,1)}, bf16[256,2048]{1,0:T(8,128)(2,1)S(1)}, u32[]{:S(2)}) copy-start(bf16[256,2048]{1,0:T(8,128)(2,1)S(1)} %collective-permute-done.2.rest_6_) | copy-start | bytes 3145732
  111.9 63.0 %collective-permute-start.3 = (f32[512,2048]{1,0:T(8,128)}, f32[512,2048]{1,0:T(8,128)}, u32[]{:S(2)}, u32[]{:S(2)}) collective-permute-start(f32[512,2048]{1,0:T(8,128)} %get-tuple-element.43), channel_id=1, source_target_pairs={{0,1},{1,0},{2,3},{3,2},{4,5},{5,4},{6,7},{7,6},{8,9},{9,8},{10,11... | collective-permute-start | bytes 12582920 | tf_op jit(solution)/shard_map/ppermute | solution.py:674
  111.9 24.4 %collective-permute-start.7 = (bf16[256,2048]{1,0:T(8,128)(2,1)S(1)}, bf16[256,2048]{1,0:T(8,128)(2,1)}, u32[]{:S(2)}, u32[]{:S(2)}) collective-permute-start(bf16[256,2048]{1,0:T(8,128)(2,1)S(1)} %collective-permute-done.2.rest_6_), channel_id=1, source_target_pairs={{0,2},{1,3},{2,0},{3,1},{4,6},{5,7},{6,4},{7,5},{8,10},{9,11},{10,... | collective-permute-start | bytes 3145736 | tf_op jit(solution)/shard_map/ppermute | solution.py:674
  113.2 46.4 %collective-permute-start.6 = (bf16[256,2048]{1,0:T(8,128)(2,1)S(1)}, bf16[256,2048]{1,0:T(8,128)(2,1)}, u32[]{:S(2)}, u32[]{:S(2)}) collective-permute-start(bf16[256,2048]{1,0:T(8,128)(2,1)S(1)} %collective-permute-done.2.rest_6_), channel_id=1, source_target_pairs={{0,1},{1,0},{2,3},{3,2},{4,5},{5,4},{6,7},{7,6},{8,9},{9,8},{10,11... | collective-permute-start | bytes 3145736 | tf_op jit(solution)/shard_map/ppermute | solution.py:674
  113.6 46.0 %collective-permute-start.4 = (bf16[256,2048]{1,0:T(8,128)(2,1)S(1)}, bf16[256,2048]{1,0:T(8,128)(2,1)}, u32[]{:S(2)}, u32[]{:S(2)}) collective-permute-start(bf16[256,2048]{1,0:T(8,128)(2,1)S(1)} %collective-permute-done.rest_4_), channel_id=1, source_target_pairs={{0,1},{1,0},{2,3},{3,2},{4,5},{5,4},{6,7},{7,6},{8,9},{9,8},{10,11... | collective-permute-start | bytes 3145736 | tf_op jit(solution)/shard_map/ppermute | solution.py:674
  113.7 45.9 %collective-permute-start.5 = (bf16[256,2048]{1,0:T(8,128)(2,1)S(1)}, bf16[256,2048]{1,0:T(8,128)(2,1)}, u32[]{:S(2)}, u32[]{:S(2)}) collective-permute-start(bf16[256,2048]{1,0:T(8,128)(2,1)S(1)} %collective-permute-done.1.rest_5_), channel_id=1, source_target_pairs={{0,1},{1,0},{2,3},{3,2},{4,5},{5,4},{6,7},{7,6},{8,9},{9,8},{10,11... | collective-permute-start | bytes 3145736 | tf_op jit(solution)/shard_map/ppermute | solution.py:674
  136.3 23.3 %collective-permute-start.8 = (bf16[256,2048]{1,0:T(8,128)(2,1)}, bf16[256,2048]{1,0:T(8,128)(2,1)}, u32[]{:S(2)}, u32[]{:S(2)}) collective-permute-start(bf16[256,2048]{1,0:T(8,128)(2,1)} %collective-permute-done.7.rest_3_), channel_id=1, source_target_pairs={{0,1},{1,0},{2,3},{3,2},{4,5},{5,4},{6,7},{7,6},{8,9},{9,8},{10,11... | collective-permute-start | bytes 3145736 | tf_op jit(solution)/shard_map/ppermute | solution.py:674
  205.0 104.0 %collective-permute-start.9 = (f32[256,2048]{1,0:T(8,128)}, f32[256,2048]{1,0:T(8,128)}, u32[]{:S(2)}, u32[]{:S(2)}) collective-permute-start(f32[256,2048]{1,0:T(8,128)} %get-tuple-element.56), channel_id=1, source_target_pairs={{0,2},{1,3},{2,0},{3,1},{4,6},{5,7},{6,4},{7,5},{8,10},{9,11},{10,... | collective-permute-start | bytes 6291464 | tf_op jit(solution)/shard_map/ppermute | solution.py:674
  205.4 103.6 %copy-start.1 = (f32[256,2048]{1,0:T(8,128)S(1)}, f32[256,2048]{1,0:T(8,128)}, u32[]{:S(2)}) copy-start(f32[256,2048]{1,0:T(8,128)} %get-tuple-element.50) | copy-start | bytes 6291460
  205.4 103.6 %copy-start.2 = (bf16[256,1024]{1,0:T(8,128)(2,1)S(1)}, bf16[256,1024]{1,0:T(8,128)(2,1)}, u32[]{:S(2)}) copy-start(bf16[256,1024]{1,0:T(8,128)(2,1)} %x_ref.3) | copy-start | bytes 1572868
  205.4 106.0 %copy-start.3 = (bf16[256,1024]{1,0:T(8,128)(2,1)S(1)}, bf16[256,1024]{1,0:T(8,128)(2,1)}, u32[]{:S(2)}) copy-start(bf16[256,1024]{1,0:T(8,128)(2,1)} %param.16) | copy-start | bytes 1572868
  205.4 106.0 %copy-start.8 = (bf16[1024,32]{0,1:T(8,128)(2,1)S(1)}, bf16[1024,32]{0,1:T(8,128)(2,1)}, u32[]{:S(2)}) copy-start(bf16[1024,32]{0,1:T(8,128)(2,1)} %param.11) | copy-start | bytes 196612
  205.4 106.0 %copy-start.9 = (bf16[32,256]{1,0:T(8,128)(2,1)S(1)}, bf16[32,256]{1,0:T(8,128)(2,1)}, u32[]{:S(2)}) copy-start(bf16[32,256]{1,0:T(8,128)(2,1)} %get-tuple-element.57) | copy-start | bytes 49156
  205.4 108.6 %copy-start.7 = (f32[32,1024]{1,0:T(8,128)S(1)}, f32[32,1024]{1,0:T(8,128)}, u32[]{:S(2)}) copy-start(f32[32,1024]{1,0:T(8,128)} %get-tuple-element.63) | copy-start | bytes 393220
